TPU v7x, 32 devices: a whole 2x2x4 slice. The times are simulated.
32 devices in a mesh: groups: 2 (over y), seq: 4 (over z), head: 2 (over x), cfg: 2 (over core).
Axes of the slice: x: 2, y: 2, z: 4, core: 2. Of those that a mesh axis runs over, the one named last changes fastest.
Arguments:
- queries: bfloat16 [2, 1024, 3072], P('cfg', ('groups', 'seq'), 'head'), parts along dimension 1, may hold values from -60 to 60
- keys: bfloat16 [2, 1024, 3072], P('cfg', ('groups', 'seq'), 'head'), parts along dimension 1, may hold values from -3 to 3
- values: bfloat16 [2, 1024, 3072], P('cfg', ('groups', 'seq'), 'head'), parts along dimension 1, may hold values from -6 to 6
- band_mask: int32 [48, 4, 4], P(('groups', 'head')), parts along dimension 0, may hold values from 0 to 1, as said below
- out_weight: bfloat16 [3072, 3072], P('head', 'cfg'), may hold values from -0.109375 to 0.109375
- guidance: float32 [1], replicated, may hold values from 3 to 8
Outputs:
- projected: bfloat16 [1024, 3072], P(('groups', 'seq'), ('cfg', 'head')), parts along dimension 0
There are 2 independent parts, one for each index of `groups`. A program takes and returns all parts, laid end to end along the dimension named above; an argument that names none is the same for every part. Nothing has to cross between parts.
Inputs may be any that keep to these rules, and one draw needn't show every extreme that they name: `band_mask`: densities are drawn per head.
All inputs are finite; a program needn't handle non-finite values.
Results may differ from a plain program's by a relative error of at most 0.02.
Values may be sent and summed in bfloat16 or wider, within the bound.
No kernel may reach another device: no remote copies, remote signals or barrier semaphores. Data moves between devices by JAX's collectives and lax.ppermute only.
A program may use at most 128 MiB of HBM per device.

v0:
```python
import jax
import jax.numpy as jnp
from jax import lax
from jax.sharding import PartitionSpec as P

HD = 128


def swapped(array, axis, bit):
    return lax.ppermute(array, axis, [(i, i ^ 1 << bit) for i in range(lax.axis_size(axis))])


def shards(queries, keys, values, band_mask, out_weight, guidance):
    own_q = queries[0]
    own_k = keys[0]
    own_v = values[0]
    q_rows = own_q.shape[0]
    kv_rows = own_k.shape[0]
    local_heads = own_q.shape[1] // HD
    tiles = lax.axis_size("seq")
    place = lax.axis_index("seq")
    scale = HD ** (-0.5)
    bands = jnp.arange(tiles)
    ident = (bands[:, None] == bands[None, :]).astype(jnp.int32)
    allowed = band_mask + ident[None] > 0
    q_heads = own_q.reshape(q_rows, local_heads, HD)
    my_row = lax.dynamic_index_in_dim(allowed, place, 1, keepdims=False)
    k_piece = lax.all_gather(own_k, "seq", axis=0, tiled=True)
    v_piece = lax.all_gather(own_v, "seq", axis=0, tiled=True)
    count = k_piece.shape[0]
    band = jnp.arange(count) // kv_rows
    onehot = band[:, None] == bands[None, :]
    keymask = jnp.any(onehot[None] & my_row[:, None, :], axis=-1)
    top = jnp.full((local_heads, q_rows), -1e30, jnp.float32)
    k_heads = k_piece.reshape(count, local_heads, HD)
    v_heads = v_piece.reshape(count, local_heads, HD)
    scores = (
        jnp.einsum("qhd,khd->hqk", q_heads, k_heads, preferred_element_type=jnp.float32) * scale
    )
    scores = jnp.where(keymask[:, None, :], scores, -1e30)
    new_top = jnp.maximum(top, jnp.max(scores, axis=-1))
    expo = jnp.where(keymask[:, None, :], jnp.exp(scores - new_top[..., None]), 0.0)
    total = jnp.sum(expo, axis=-1)
    accum = jnp.einsum(
        "hqk,khd->hqd", expo.astype(jnp.bfloat16), v_heads, preferred_element_type=jnp.float32
    )
    top, total, accum = (new_top, total, accum)
    attn = accum / total[..., None]
    own_rows = jnp.transpose(attn, (1, 0, 2)).reshape(q_rows, local_heads * HD).astype(jnp.bfloat16)
    partner = swapped(own_rows, "cfg", 0)
    first_copy = lax.axis_index("cfg") == 0
    cond = jnp.where(first_copy, own_rows, partner).astype(jnp.float32)
    uncond = jnp.where(first_copy, partner, own_rows).astype(jnp.float32)
    guided = (uncond + guidance[0] * (cond - uncond)).astype(jnp.bfloat16)
    terms = jnp.dot(guided, out_weight, preferred_element_type=jnp.float32)
    return lax.psum_scatter(terms.astype(jnp.bfloat16), "head", scatter_dimension=1, tiled=True)


def solution(mesh):
    in_specs = (
        P("cfg", ("groups", "seq"), "head"),
        P("cfg", ("groups", "seq"), "head"),
        P("cfg", ("groups", "seq"), "head"),
        P(("groups", "head"), None, None),
        P("head", "cfg"),
        P(),
    )
    out_specs = P(("groups", "seq"), ("cfg", "head"))
    return jax.shard_map(shards, mesh=mesh, in_specs=in_specs, out_specs=out_specs, check_vma=False)
```

profile of v0, /device:TPU:0, one launch (start us, length us, event | category | flops | bytes accessed | tf_op | source)
XLA Modules:
  0.0 115.7 jit_solution(17461585019683338702)
XLA Ops:
  6.5 0.0 all-gather.5.cloned.1.call-start
  6.5 1.9 %copy.18 = bf16[1,128,1536]{1,2,0:T(8,128)(2,1)} copy(bf16[1,128,1536]{2,1,0:T(8,128)(2,1)} %param.7) | data formatting | bytes 786432 | tf_op args[1]
  8.4 0.0 all-gather.5.cloned.1.call-update
  8.5 0.0 all-gather.7.cloned.1.call-start
  8.5 0.7 all-gather.7.cloned.1.call-update
  9.2 0.0 reduce-scatter.2.cloned.1.call-start
  9.3 0.8 fusion.31
  10.1 0.1 copy.16
  10.2 1.2 %copy.17 = bf16[1,128,1536]{1,2,0:T(8,128)(2,1)S(1)} copy(bf16[1,128,1536]{2,1,0:T(8,128)(2,1)} %param.6) | data formatting | bytes 786432 | tf_op args[0]
  11.4 0.1 and_reduce_fusion
  11.6 37.8 %all-gather.5.cloned.1.call-done = bf16[1,512,1536]{1,2,0:T(8,128)(2,1)} async-done(((bf16[1,128,1536]{1,2,0:T(8,128)(2,1)}), bf16[1,512,1536]{1,2,0:T(8,128)(2,1)}) %all-gather.5.cloned.1.call-update) | async-done | bytes 1572880 | tf_op jit(solution)/shard_map/all_gather | solution.py:28
  49.3 2.2 %fusion = (f32[12,128]{1,0:T(8,128)S(1)}, f32[12,128,512]{2,1,0:T(8,128)S(1)}) fusion(pred[12,512]{1,0:T(8,128)(4,1)S(1)} %and_reduce_fusion, bf16[128,12,128]{0,2,1:T(8,128)(2,1)S(1)} %bitcast.20, bf16[512,12,128]{0,2,1:T(8,128)(2,1)} %bitcast.21), kind=kOutput, calls=%fused_computation.2 | convolution fusion | flops 203684352 | bytes 5124096 | tf_op jit(solution)/shard_map/qhd,khd->hqk/dot_general | solution.py:38
  51.5 1.6 %fusion.1 = f32[12,128]{1,0:T(8,128)} fusion(f32[12,128,512]{2,1,0:T(8,128)S(1)} %get-tuple-element.6, f32[12,128]{1,0:T(8,128)S(1)} %broadcast_maximum_fusion, pred[12,512]{1,0:T(8,128)(4,1)S(1)} %and_reduce_fusion), kind=kLoop, calls=%fused_computation.4 | loop fusion | flops 3930624 | bytes 3164160 | tf_op jit(solution)/shard_map/reduce_sum | solution.py:43
  53.1 33.1 %all-gather.7.cloned.1.call-done = bf16[1,512,1536]{2,1,0:T(8,128)(2,1)} async-done(((bf16[1,128,1536]{2,1,0:T(8,128)(2,1)}), bf16[1,512,1536]{2,1,0:T(8,128)(2,1)}) %all-gather.7.cloned.1.call-update) | async-done | bytes 1572880 | tf_op jit(solution)/shard_map/all_gather | solution.py:29
  86.2 2.6 %copy.21 = bf16[1,512,1536]{1,2,0:T(8,128)(2,1)} copy(bf16[1,512,1536]{2,1,0:T(8,128)(2,1)} %all-gather.7.cloned.1.call-done) | data formatting | bytes 3145728 | tf_op jit(solution)/shard_map/all_gather | solution.py:29
  88.8 2.4 %fusion.16 = bf16[128,12,128]{0,2,1:T(8,128)(2,1)S(1)} fusion(bf16[512,12,128]{0,2,1:T(8,128)(2,1)} %bitcast.19, f32[12,128,512]{2,1,0:T(8,128)S(1)} %get-tuple-element.6, f32[12,128]{1,0:T(8,128)S(1)} %broadcast_maximum_fusion, pred[12,512]{1,0:T(8,128)(4,1)S(1)} %and_reduce_fusion, f32[128,12]{0,1:T(8,128)} %bitcast.24), kind=kOutput, calls=%fused_computation.16 | convolution fusion | flops 205651968 | bytes 5130240 | tf_op jit(solution)/shard_map/hqk,khd->hqd/dot_general | solution.py:44
  91.2 0.1 collective-permute-start
  91.9 1.1 collective-permute-done
  93.0 3.9 %convolution_convert_fusion = bf16[128,1536]{1,0:T(8,128)(2,1)} fusion(bf16[1536,1536]{1,0:T(8,128)(2,1)} %param.10, bf16[128,1536]{0,1:T(8,128)(2,1)S(1)} %bitcast.23, bf16[128,1536]{0,1:T(8,128)(2,1)S(1)} %collective-permute-done, f32[]{:T(128)} %bitcast.18, pred[]{:T(512)S(6)} %eq.37), kind=kOutput, calls=%fused_computation.3 | convolution fusion | flops 605749248 | bytes 5898245 | tf_op jit(solution)/shard_map/dot_general | solution.py:55
  96.9 0.0 reduce-scatter.2.cloned.1.call-update
  96.9 12.2 %reduce-scatter.2.cloned.1.call-done = bf16[128,768]{1,0:T(8,128)(2,1)} async-done(((bf16[128,1536]{1,0:T(8,128)(2,1)}), bf16[128,768]{1,0:T(8,128)(2,1)}) %reduce-scatter.2.cloned.1.call-update) | async-done | bytes 196624 | tf_op jit(solution)/shard_map/reduce_scatter | solution.py:56
  (5 shorter events, 0.0 us)
Async XLA Ops:
  6.5 42.8 %all-gather.5.cloned.1.call-start = ((), (), s32[]{:S(2)}) async-start(), calls=%async_computation.2 | async-start | bytes 1966080 | tf_op jit(solution)/shard_map/all_gather | solution.py:28
  8.5 77.7 %all-gather.7.cloned.1.call-start = ((), (), s32[]{:S(2)}) async-start(), calls=%async_computation.3 | async-start | bytes 1966080 | tf_op jit(solution)/shard_map/all_gather | solution.py:29
  9.2 99.9 %reduce-scatter.2.cloned.1.call-start = ((), (), s32[]{:S(2)}) async-start(), calls=%async_computation.1 | async-start | bytes 589824 | tf_op jit(solution)/shard_map/reduce_scatter | solution.py:56
  91.2 1.8 %collective-permute-start = (bf16[128,1536]{0,1:T(8,128)(2,1)S(1)}, bf16[128,1536]{0,1:T(8,128)(2,1)S(1)}, u32[]{:S(2)}, u32[]{:S(2)}) collective-permute-start(bf16[128,1536]{0,1:T(8,128)(2,1)S(1)} %bitcast.22), channel_id=1, source_target_pairs={{0,1},{1,0},{2,3},{3,2},{4,5},{5,4},{6,7},{7,6},{8,9},{9,8},{10,11... | collective-permute-start | bytes 1179656 | tf_op jit(solution)/shard_map/ppermute | solution.py:10
Sparse Core Ops, SparseCore 0:
  8.9 40.3 all-gather.4
  50.9 35.2 all-gather.6
  97.0 12.0 reduce-scatter.1
where the time goes:
time: 116 us
  waiting for transfers between devices  84.8 us (73%)
  between operations  13.8 us (12%)
  matrix products  8.47 us (7%)
  local copies, waits for them, and re-layouts  5.84 us (5%)
  other arithmetic  2.52 us (2%)
    all_gather x1, waiting for transfers between devices, shards(): k_piece = lax.all_gather(own_k, 'seq', axis=0, tiled=True)  37.8 us
    all_gather x1, waiting for transfers between devices, shards(): v_piece = lax.all_gather(own_v, 'seq', axis=0, tiled=True)  33.1 us
    reduce_scatter x1, waiting for transfers between devices, shards(): lax.psum_scatter(terms.astype(jnp.bfloat16), 'head', scatter_dimension=1,...  12.2 us
    dot_general x1, matrix products, shards(): terms = jnp.dot(guided, out_weight, preferred_element_type=jnp.float32)  3.91 us
    unnamed x2, local copies, waits for them, and re-layouts  3.12 us
    all_gather x1, local copies, waits for them, and re-layouts, shards(): v_piece = lax.all_gather(own_v, 'seq', axis=0, tiled=True)  2.6 us
    dot_general x1, matrix products, shards(): jnp.einsum('hqk,khd->hqd', expo.astype(jnp.bfloat16), v_heads, preferred_...  2.39 us
  transfers between devices with their start and end apart: 4, of which 4 were waited for; matrix products, arithmetic and copies ran while one was open for 5% of the time, Pallas kernels for 0%

commit v1 on v0

--- a/solution.py
+++ b/solution.py
@@ -1,16 +1,191 @@
+import functools
+
 import jax
 import jax.numpy as jnp
 from jax import lax
+from jax.experimental import pallas as pl
+from jax.experimental.pallas import tpu as pltpu
 from jax.sharding import PartitionSpec as P
 
 HD = 128
-
-
-def swapped(array, axis, bit):
-    return lax.ppermute(array, axis, [(i, i ^ 1 << bit) for i in range(lax.axis_size(axis))])
-
-
-def shards(queries, keys, values, band_mask, out_weight, guidance):
+MIB = 1 << 20
+
+
+def swapped(array, axis, bits):
+    return lax.ppermute(array, axis, [(i, i ^ bits) for i in range(lax.axis_size(axis))])
+
+
+def vmem(count):
+    return [pl.BlockSpec(memory_space=pltpu.VMEM)] * count
+
+
+def call(body, outs, args, flops, limit=16):
+    moved = sum(a.size * a.dtype.itemsize for a in [*args, *outs])
+    return pl.pallas_call(
+        body,
+        out_shape=outs,
+        in_specs=vmem(len(args)),
+        out_specs=vmem(len(outs)),
+        compiler_params=pltpu.CompilerParams(vmem_limit_bytes=limit * MIB),
+        cost_estimate=pl.CostEstimate(flops=flops, bytes_accessed=moved, transcendentals=0),
+    )(*args)
+
+
+def columns(head, count):
+    return pl.ds(pl.multiple_of(head * HD, HD), count * HD)
+
+
+def pack_body(slots, per, chunks, q_ref, k_ref, v_ref, *outs):
+    place = lax.axis_index("seq")
+    at = 0
+    for first, count in chunks:
+        for slot in range(slots):
+            cols = columns((place ^ slot) * per + first, count)
+            for part, ref in enumerate((q_ref, k_ref, v_ref)):
+                outs[at][part] = ref[:, cols]
+            at += 1
+
+
+def attend_body(slots, first, count, scale, bias_ref, *refs):
+    blocks, (keep_ref, send_ref) = refs[:slots], refs[slots:]
+    rows = blocks[0].shape[1]
+    half = rows // 2
+    low = lax.axis_index("cfg") == 0
+    for head in range(count):
+        cols = slice(head * HD, (head + 1) * HD)
+        keys = jnp.concatenate([b[1, :, cols] for b in blocks], axis=0)
+        values = jnp.concatenate([b[2, :, cols] for b in blocks], axis=0)
+        for slot in range(slots):
+            scores = lax.dot_general(
+                blocks[slot][0, :, cols], keys, (((1,), (1,)), ((), ())),
+                preferred_element_type=jnp.float32,
+            )
+            line = (first + head) * slots + slot
+            scores = scores * scale + bias_ref[line : line + 1, :]
+            top = jnp.max(scores, axis=1, keepdims=True)
+            expo = jnp.exp(scores - top)
+            total = jnp.sum(expo, axis=1, keepdims=True)
+            out = jnp.dot(expo.astype(jnp.bfloat16), values, preferred_element_type=jnp.float32)
+            out = (out / total).astype(jnp.bfloat16)
+            keep_ref[slot, :, cols] = jnp.where(low, out[:half], out[half:])
+            send_ref[slot, :, cols] = jnp.where(low, out[half:], out[:half])
+
+
+def guide_body(slots, scale_ref, own_ref, other_ref, *outs):
+    low = lax.axis_index("cfg") == 0
+    strength = scale_ref[0:1, 0:1]
+    for slot in range(slots):
+        own = own_ref[slot].astype(jnp.float32)
+        other = other_ref[slot].astype(jnp.float32)
+        cond = jnp.where(low, own, other)
+        uncond = jnp.where(low, other, own)
+        outs[slot][...] = (uncond + strength * (cond - uncond)).astype(jnp.bfloat16)
+
+
+def join_body(slots, *refs):
+    ins, out = refs[:slots], refs[slots]
+    for slot in range(slots):
+        out[slot] = ins[slot][...]
+
+
+def project_body(slots, per, chunks, mine_side, w_ref, *refs):
+    pairs, (out_ref, wide_ref) = refs[:-2], refs[-2:]
+    place, core, side = lax.axis_index("seq"), lax.axis_index("cfg"), lax.axis_index("head")
+    half = out_ref.shape[0] // 2
+    width = out_ref.shape[1]
+    for index, (first, count) in enumerate(chunks):
+        mine, theirs = pairs[2 * index], pairs[2 * index + 1]
+        for slot in range(slots):
+            cols = columns((place ^ slot) * per + first, count)
+            wide_ref[pl.ds(pl.multiple_of(core * half, half), half), cols] = mine[slot]
+            wide_ref[pl.ds(pl.multiple_of((1 - core) * half, half), half), cols] = theirs[slot]
+    block = side if mine_side else 1 - side
+    weights = w_ref[:, pl.ds(pl.multiple_of(block * width, HD), width)]
+    out_ref[...] = jnp.dot(wide_ref[...], weights, preferred_element_type=jnp.float32).astype(out_ref.dtype)
+
+
+def by_heads(queries, keys, values, band_mask, out_weight, guidance):
+    own_q, own_k, own_v = queries[0], keys[0], values[0]
+    rows, wide = own_q.shape
+    slots = lax.axis_size("seq")
+    place = lax.axis_index("seq")
+    per = wide // HD // slots
+    chunks = [(0, per)] if per < 2 else [(0, per - per // 3), (per - per // 3, per // 3)]
+    chunks = [c for c in chunks if c[1] > 0]
+    half = rows // 2
+    bf16, f32 = jnp.bfloat16, jnp.float32
+
+    packed = call(
+        functools.partial(pack_body, slots, per, chunks),
+        [jax.ShapeDtypeStruct((3, rows, c * HD), bf16) for _, c in chunks for _ in range(slots)],
+        [own_q, own_k, own_v],
+        0,
+    )
+    order = sorted(range(1, slots), reverse=True)
+    received = []
+    for index in range(len(chunks)):
+        got = {0: packed[index * slots]}
+        for slot in order:
+            got[slot] = swapped(packed[index * slots + slot], "seq", slot)
+        received.append([got[s] for s in range(slots)])
+
+    tiles = jnp.arange(slots)
+    mine = lax.dynamic_slice_in_dim(band_mask, place * per, per, 0)
+    pick = ((place ^ tiles)[:, None] == tiles[None, :])[None, :, None, :, None] & (
+        ((place ^ tiles)[:, None] == tiles[None, :])[None, None, :, None, :]
+    )
+    listed = jnp.sum(jnp.where(pick, mine[:, None, None], 0), axis=(3, 4))
+    allowed = (listed + jnp.eye(slots, dtype=jnp.int32)[None]) > 0
+    bias = jnp.where(allowed, 0.0, -1e30).astype(f32)
+    bias = jnp.repeat(bias.reshape(per * slots, slots), own_k.shape[0], axis=1)
+    strength = jnp.broadcast_to(guidance.reshape(1, 1), (8, HD))
+
+    shared = []
+    for (first, count), blocks in zip(chunks, received):
+        shape = jax.ShapeDtypeStruct((slots, half, count * HD), bf16)
+        keep, send = call(
+            functools.partial(attend_body, slots, first, count, HD ** (-0.5)),
+            [shape, shape],
+            [bias, *blocks],
+            4 * count * (slots * rows) ** 2 * HD,
+        )
+        other = swapped(send, "cfg", 1)
+        guided = call(
+            functools.partial(guide_body, slots),
+            [jax.ShapeDtypeStruct((half, count * HD), bf16)] * slots,
+            [strength, keep, other],
+            8 * slots * half * count * HD,
+        )
+        back = {0: guided[0]}
+        for slot in order:
+            back[slot] = swapped(guided[slot], "seq", slot)
+        (mine,) = call(
+            functools.partial(join_body, slots), [shape], [back[s] for s in range(slots)], 0
+        )
+        shared += [mine, swapped(mine, "cfg", 1)]
+
+    width = out_weight.shape[1] // 2
+
+    def project(mine_side, dtype):
+        return pl.pallas_call(
+            functools.partial(project_body, slots, per, chunks, mine_side),
+            out_shape=jax.ShapeDtypeStruct((rows, width), dtype),
+            in_specs=vmem(1 + len(shared)),
+            out_specs=vmem(1)[0],
+            scratch_shapes=[pltpu.VMEM((rows, wide), bf16)],
+            compiler_params=pltpu.CompilerParams(vmem_limit_bytes=16 * MIB),
+            cost_estimate=pl.CostEstimate(
+                flops=2 * rows * wide * width,
+                bytes_accessed=wide * width * 2,
+                transcendentals=0,
+            ),
+        )(out_weight, *shared)
+
+    theirs = swapped(project(False, bf16), "head", 1)
+    return (project(True, f32) + theirs.astype(f32)).astype(bf16)
+
+
+def by_bands(queries, keys, values, band_mask, out_weight, guidance):
     own_q = queries[0]
     own_k = keys[0]
     own_v = values[0]
@@ -31,29 +206,37 @@
     band = jnp.arange(count) // kv_rows
     onehot = band[:, None] == bands[None, :]
     keymask = jnp.any(onehot[None] & my_row[:, None, :], axis=-1)
-    top = jnp.full((local_heads, q_rows), -1e30, jnp.float32)
     k_heads = k_piece.reshape(count, local_heads, HD)
     v_heads = v_piece.reshape(count, local_heads, HD)
     scores = (
         jnp.einsum("qhd,khd->hqk", q_heads, k_heads, preferred_element_type=jnp.float32) * scale
     )
     scores = jnp.where(keymask[:, None, :], scores, -1e30)
-    new_top = jnp.maximum(top, jnp.max(scores, axis=-1))
-    expo = jnp.where(keymask[:, None, :], jnp.exp(scores - new_top[..., None]), 0.0)
+    top = jnp.max(scores, axis=-1)
+    expo = jnp.where(keymask[:, None, :], jnp.exp(scores - top[..., None]), 0.0)
     total = jnp.sum(expo, axis=-1)
     accum = jnp.einsum(
         "hqk,khd->hqd", expo.astype(jnp.bfloat16), v_heads, preferred_element_type=jnp.float32
     )
-    top, total, accum = (new_top, total, accum)
     attn = accum / total[..., None]
     own_rows = jnp.transpose(attn, (1, 0, 2)).reshape(q_rows, local_heads * HD).astype(jnp.bfloat16)
-    partner = swapped(own_rows, "cfg", 0)
+    partner = swapped(own_rows, "cfg", 1)
     first_copy = lax.axis_index("cfg") == 0
     cond = jnp.where(first_copy, own_rows, partner).astype(jnp.float32)
     uncond = jnp.where(first_copy, partner, own_rows).astype(jnp.float32)
     guided = (uncond + guidance[0] * (cond - uncond)).astype(jnp.bfloat16)
     terms = jnp.dot(guided, out_weight, preferred_element_type=jnp.float32)
     return lax.psum_scatter(terms.astype(jnp.bfloat16), "head", scatter_dimension=1, tiled=True)
+
+
+def shards(queries, keys, values, band_mask, out_weight, guidance):
+    slots = lax.axis_size("seq")
+    heads = queries.shape[2] // HD
+    rows = queries.shape[1]
+    fits = heads % slots == 0 and slots & (slots - 1) == 0 and rows == keys.shape[1]
+    fits = fits and rows % 32 == 0 and lax.axis_size("cfg") == 2 and lax.axis_size("head") == 2
+    plan = by_heads if fits else by_bands
+    return plan(queries, keys, values, band_mask, out_weight, guidance)
 
 
 def solution(mesh):

time: 116 us -> 63.8 us (0.55)
  waiting for transfers between devices: 84.8 us -> 28.6 us
  starting transfers between devices: 0.15 us -> 21.9 us
  between operations: 13.8 us -> 0.84 us
  matrix products: 8.47 us -> 0 us
  Pallas kernels: 0 us -> 4.76 us
    all_gather x2 -> x0, waiting for transfers between devices: 70.8 us -> none  [the longest x1 37.8 us: shards(): k_piece = lax.all_gather(own_k, 'seq', axis=0, tiled=True)]
    ppermute x1 -> x17, waiting for transfers between devices: 1.06 us -> 28.6 us  [swapped(): lax.ppermute(array, axis, [(i, i ^ bits) for i in range(lax.axis_size(axi...]
    ppermute x1 -> x17, starting transfers between devices: 0.07 us -> 21.9 us  [swapped(): lax.ppermute(array, axis, [(i, i ^ bits) for i in range(lax.axis_size(axi...]
    reduce_scatter x1 -> x0, waiting for transfers between devices: 12.2 us -> none  [shards(): lax.psum_scatter(terms.astype(jnp.bfloat16), 'head', scatter_dimension=1,...]
    dot_general x3 -> x0, matrix products: 8.47 us -> none  [the longest x1 3.91 us: shards(): terms = jnp.dot(guided, out_weight, preferred_element_type=jnp.float32)]
    pallas_call x0 -> x9, Pallas kernels: none -> 4.76 us  [the longest x7 3.75 us: call(): pl.pallas_call(body, out_shape=outs, in_specs=vmem(len(args)), out_specs=...]
    all_gather x1 -> x0, local copies, waits for them, and re-layouts: 2.6 us -> none  [shards(): v_piece = lax.all_gather(own_v, 'seq', axis=0, tiled=True)]
    unnamed x2 -> x12, local copies, waits for them, and re-layouts: 3.12 us -> 5.36 us
  transfers between devices with their start and end apart: 4 -> 17, of which waited for: 4 -> 8; matrix products, arithmetic and copies ran while one was open for 5% -> 2% of each run, Pallas kernels for 0% -> 3%
where the time goes in v1:
time: 63.8 us; the launch traced here: 63.6 us
  waiting for transfers between devices  28.6 us (45%)
  starting transfers between devices  21.9 us (34%)
  local copies, waits for them, and re-layouts  5.63 us (9%)
  Pallas kernels  4.76 us (7%)
  other arithmetic  1.83 us (3%)
  between operations  0.84 us (1%)
    ppermute x17, waiting for transfers between devices, swapped(): lax.ppermute(array, axis, [(i, i ^ bits) for i in range(lax.axis_size(axi...  28.6 us
    ppermute x17, starting transfers between devices, swapped(): lax.ppermute(array, axis, [(i, i ^ bits) for i in range(lax.axis_size(axi...  21.9 us
    unnamed x12, local copies, waits for them, and re-layouts  5.36 us
    pallas_call x7, Pallas kernels, call(): pl.pallas_call(body, out_shape=outs, in_specs=vmem(len(args)), out_specs=...  3.75 us
  transfers between devices with their start and end apart: 17, of which 8 were waited for; matrix products, arithmetic and copies ran while one was open for 2% of the time, Pallas kernels for 3%

profile of v1, /device:TPU:0, one launch (start us, length us, event | category | flops | bytes accessed | tf_op | source)
XLA Modules:
  0.0 63.6 jit_solution(14848924561194543569)
XLA Ops:
  0.0 1.0 %copy-done.2 = bf16[1,128,1536]{2,1,0:T(8,128)(2,1)S(1)} copy-done((bf16[1,128,1536]{2,1,0:T(8,128)(2,1)S(1)}, bf16[1,128,1536]{2,1,0:T(8,128)(2,1)}, u32[]{:S(2)}) %copy-start.2) | copy-done | bytes 393240
  1.0 1.0 %copy-done.3 = bf16[1,128,1536]{2,1,0:T(8,128)(2,1)S(1)} copy-done((bf16[1,128,1536]{2,1,0:T(8,128)(2,1)S(1)}, bf16[1,128,1536]{2,1,0:T(8,128)(2,1)}, u32[]{:S(2)}) %copy-start.3) | copy-done | bytes 393240
  2.0 1.0 %copy-done.4 = bf16[1,128,1536]{2,1,0:T(8,128)(2,1)S(1)} copy-done((bf16[1,128,1536]{2,1,0:T(8,128)(2,1)S(1)}, bf16[1,128,1536]{2,1,0:T(8,128)(2,1)}, u32[]{:S(2)}) %copy-start.4) | copy-done | bytes 393240
  3.0 0.1 shard_map.64
  3.1 3.1 %collective-permute-start = (bf16[3,128,256]{2,1,0:T(8,128)(2,1)S(1)}, bf16[3,128,256]{2,1,0:T(8,128)(2,1)S(1)}, u32[]{:S(2)}, u32[]{:S(2)}) collective-permute-start(bf16[3,128,256]{2,1,0:T(8,128)(2,1)S(1)} %get-tuple-element.26), channel_id=1, source_target_pairs={{0,4},{4,0},{8,12},{12,8},{1,5},{5,1},{9,13},{13,9},{2,6},{6,2},{1... | collective-permute-start | bytes 589832 | tf_op jit(solution)/shard_map/ppermute | solution.py:15
  6.2 2.6 %collective-permute-start.1 = (bf16[3,128,256]{2,1,0:T(8,128)(2,1)S(1)}, bf16[3,128,256]{2,1,0:T(8,128)(2,1)S(1)}, u32[]{:S(2)}, u32[]{:S(2)}) collective-permute-start(bf16[3,128,256]{2,1,0:T(8,128)(2,1)S(1)} %get-tuple-element.27), channel_id=1, source_target_pairs={{0,8},{4,12},{8,0},{12,4},{1,9},{5,13},{9,1},{13,5},{2,10},{6,14},... | collective-permute-start | bytes 589832 | tf_op jit(solution)/shard_map/ppermute | solution.py:15
  8.9 0.1 copy.11
  9.2 0.9 %select_reduce_fusion = s32[3,4,4]{2,1,0:T(4,128)S(1)} fusion(s32[3,4,4]{2,1,0:T(4,128)S(1)} %copy.11, pred[4,4,4,4]{3,2,1,0:T(4,128)(4,1)S(1)} %broadcast_and_fusion), kind=kLoop, calls=%fused_computation.1 | loop fusion | flops 1488 | bytes 640 | tf_op jit(solution)/shard_map/reduce_sum | solution.py:137
  10.3 4.3 %collective-permute-done.refs_1_ = bf16[3,128,256]{2,1,0:T(8,128)(2,1)S(1)} collective-permute-done((bf16[3,128,256]{2,1,0:T(8,128)(2,1)S(1)}, bf16[3,128,256]{2,1,0:T(8,128)(2,1)S(1)}, u32[]{:S(2)}, u32[]{:S(2)}) %collective-permute-start) | collective-permute-done | bytes 196640 | tf_op jit(solution)/shard_map/ppermute | solution.py:15
  14.6 8.7 %collective-permute-done.1.refs_2_ = bf16[3,128,256]{2,1,0:T(8,128)(2,1)S(1)} collective-permute-done((bf16[3,128,256]{2,1,0:T(8,128)(2,1)S(1)}, bf16[3,128,256]{2,1,0:T(8,128)(2,1)S(1)}, u32[]{:S(2)}, u32[]{:S(2)}) %collective-permute-start.1) | collective-permute-done | bytes 196640 | tf_op jit(solution)/shard_map/ppermute | solution.py:15
  23.4 2.3 %shard_map.65 = (bf16[4,64,256]{2,1,0:T(8,128)(2,1)S(1)}, bf16[4,64,256]{2,1,0:T(8,128)(2,1)S(1)}) custom-call(f32[12,512]{1,0:T(8,128)S(1)} %bitcast.11, bf16[3,128,256]{2,1,0:T(8,128)(2,1)S(1)} %get-tuple-element.25.refs_0_, bf16[3,128,256]{2,1,0:T(8,128)(2,1)S(1)} %collective-permute-done.refs_1_, ...), custom_call_target="tpu_custom_call" | custom-call | flops 268435456 | bytes 1073152 | tf_op jit(solution)/shard_map/pallas_call | solution.py:24
  25.7 2.5 %collective-permute-start.10 = (bf16[3,128,128]{2,1,0:T(8,128)(2,1)S(1)}, bf16[3,128,128]{2,1,0:T(8,128)(2,1)S(1)}, u32[]{:S(2)}, u32[]{:S(2)}) collective-permute-start(bf16[3,128,128]{2,1,0:T(8,128)(2,1)S(1)} %get-tuple-element.38), channel_id=1, source_target_pairs={{0,12},{4,8},{8,4},{12,0},{1,13},{5,9},{9,5},{13,1},{2,14},{6,10},... | collective-permute-start | bytes 294920 | tf_op jit(solution)/shard_map/ppermute | solution.py:15
  28.2 2.5 %collective-permute-start.8 = (bf16[3,128,128]{2,1,0:T(8,128)(2,1)S(1)}, bf16[3,128,128]{2,1,0:T(8,128)(2,1)S(1)}, u32[]{:S(2)}, u32[]{:S(2)}) collective-permute-start(bf16[3,128,128]{2,1,0:T(8,128)(2,1)S(1)} %get-tuple-element.36), channel_id=1, source_target_pairs={{0,4},{4,0},{8,12},{12,8},{1,5},{5,1},{9,13},{13,9},{2,6},{6,2},{1... | collective-permute-start | bytes 294920 | tf_op jit(solution)/shard_map/ppermute | solution.py:15
  31.4 0.1 shard_map.66
  31.5 2.0 %collective-permute-start.4 = (bf16[64,256]{1,0:T(8,128)(2,1)S(1)}, bf16[64,256]{1,0:T(8,128)(2,1)S(1)}, u32[]{:S(2)}, u32[]{:S(2)}) collective-permute-start(bf16[64,256]{1,0:T(8,128)(2,1)S(1)} %get-tuple-element.32), channel_id=1, source_target_pairs={{0,4},{4,0},{8,12},{12,8},{1,5},{5,1},{9,13},{13,9},{2,6},{6,2},{1... | collective-permute-start | bytes 98312 | tf_op jit(solution)/shard_map/ppermute | solution.py:15
  33.5 1.1 %collective-permute-start.5 = (bf16[64,256]{1,0:T(8,128)(2,1)S(1)}, bf16[64,256]{1,0:T(8,128)(2,1)S(1)}, u32[]{:S(2)}, u32[]{:S(2)}) collective-permute-start(bf16[64,256]{1,0:T(8,128)(2,1)S(1)} %get-tuple-element.33), channel_id=1, source_target_pairs={{0,8},{4,12},{8,0},{12,4},{1,9},{5,13},{9,1},{13,5},{2,10},{6,14},... | collective-permute-start | bytes 98312 | tf_op jit(solution)/shard_map/ppermute | solution.py:15
  34.6 1.4 %collective-permute-start.6 = (bf16[64,256]{1,0:T(8,128)(2,1)S(1)}, bf16[64,256]{1,0:T(8,128)(2,1)S(1)}, u32[]{:S(2)}, u32[]{:S(2)}) collective-permute-start(bf16[64,256]{1,0:T(8,128)(2,1)S(1)} %get-tuple-element.34), channel_id=1, source_target_pairs={{0,12},{4,8},{8,4},{12,0},{1,13},{5,9},{9,5},{13,1},{2,14},{6,10},... | collective-permute-start | bytes 98312 | tf_op jit(solution)/shard_map/ppermute | solution.py:15
  36.0 4.5 %collective-permute-done.9.refs_2_ = bf16[3,128,128]{2,1,0:T(8,128)(2,1)S(1)} collective-permute-done((bf16[3,128,128]{2,1,0:T(8,128)(2,1)S(1)}, bf16[3,128,128]{2,1,0:T(8,128)(2,1)S(1)}, u32[]{:S(2)}, u32[]{:S(2)}) %collective-permute-start.9) | collective-permute-done | bytes 98336 | tf_op jit(solution)/shard_map/ppermute | solution.py:15
  40.5 1.2 %shard_map.68 = (bf16[4,64,128]{2,1,0:T(8,128)(2,1)S(1)}, bf16[4,64,128]{2,1,0:T(8,128)(2,1)S(1)}) custom-call(f32[12,512]{1,0:T(8,128)S(1)} %bitcast.12, bf16[3,128,128]{2,1,0:T(8,128)(2,1)S(1)} %get-tuple-element.35.refs_0_, bf16[3,128,128]{2,1,0:T(8,128)(2,1)S(1)} %collective-permute-done.8.refs_1_, ...), custom_call_target="tpu_custom_call" | custom-call | flops 134217728 | bytes 548864 | tf_op jit(solution)/shard_map/pallas_call | solution.py:24
  41.8 0.5 collective-permute-start.7
  42.3 0.6 %collective-permute-done.11.other_ref = bf16[4,64,128]{2,1,0:T(8,128)(2,1)S(1)} collective-permute-done((bf16[4,64,128]{2,1,0:T(8,128)(2,1)S(1)}, bf16[4,64,128]{2,1,0:T(8,128)(2,1)S(1)}, u32[]{:S(2)}, u32[]{:S(2)}) %collective-permute-start.11) | collective-permute-done | bytes 65568 | tf_op jit(solution)/shard_map/ppermute | solution.py:15
  43.1 3.0 %collective-permute-start.13 = (bf16[64,128]{1,0:T(8,128)(2,1)S(1)}, bf16[64,128]{1,0:T(8,128)(2,1)S(1)}, u32[]{:S(2)}, u32[]{:S(2)}) collective-permute-start(bf16[64,128]{1,0:T(8,128)(2,1)S(1)} %get-tuple-element.43), channel_id=1, source_target_pairs={{0,8},{4,12},{8,0},{12,4},{1,9},{5,13},{9,1},{13,5},{2,10},{6,14},... | collective-permute-start | bytes 49160 | tf_op jit(solution)/shard_map/ppermute | solution.py:15
  46.2 1.3 %collective-permute-start.14 = (bf16[64,128]{1,0:T(8,128)(2,1)S(1)}, bf16[64,128]{1,0:T(8,128)(2,1)S(1)}, u32[]{:S(2)}, u32[]{:S(2)}) collective-permute-start(bf16[64,128]{1,0:T(8,128)(2,1)S(1)} %get-tuple-element.44), channel_id=1, source_target_pairs={{0,12},{4,8},{8,4},{12,0},{1,13},{5,9},{9,5},{13,1},{2,14},{6,10},... | collective-permute-start | bytes 49160 | tf_op jit(solution)/shard_map/ppermute | solution.py:15
  47.5 0.4 collective-permute-done.13.refs_2_
  47.9 3.8 %collective-permute-done.14.refs_3_ = bf16[64,128]{1,0:T(8,128)(2,1)S(1)} collective-permute-done((bf16[64,128]{1,0:T(8,128)(2,1)S(1)}, bf16[64,128]{1,0:T(8,128)(2,1)S(1)}, u32[]{:S(2)}, u32[]{:S(2)}) %collective-permute-start.14) | collective-permute-done | bytes 16416 | tf_op jit(solution)/shard_map/ppermute | solution.py:15
  51.7 1.2 %collective-permute-done.15.refs_3_ = bf16[4,64,128]{2,1,0:T(8,128)(2,1)S(1)} collective-permute-done((bf16[4,64,128]{2,1,0:T(8,128)(2,1)S(1)}, bf16[4,64,128]{2,1,0:T(8,128)(2,1)S(1)}, u32[]{:S(2)}, u32[]{:S(2)}) %collective-permute-start.15) | collective-permute-done | bytes 65568 | tf_op jit(solution)/shard_map/ppermute | solution.py:15
  53.0 2.3 %copy-done.1 = bf16[1536,1536]{1,0:T(8,128)(2,1)S(1)} copy-done((bf16[1536,1536]{1,0:T(8,128)(2,1)S(1)}, bf16[1536,1536]{1,0:T(8,128)(2,1)}, u32[]{:S(2)}) %copy-start.1) | copy-done | bytes 4718616
  55.3 0.5 shard_map.72
  55.8 1.5 %collective-permute-start.16 = (bf16[128,768]{1,0:T(8,128)(2,1)S(1)}, bf16[128,768]{1,0:T(8,128)(2,1)S(1)}, u32[]{:S(2)}, u32[]{:S(2)}) collective-permute-start(bf16[128,768]{1,0:T(8,128)(2,1)S(1)} %shard_map.72), channel_id=1, source_target_pairs={{0,2},{2,0},{1,3},{3,1},{4,6},{6,4},{5,7},{7,5},{8,10},{10,8},{9,1... | collective-permute-start | bytes 589832 | tf_op jit(solution)/shard_map/ppermute | solution.py:15
  57.4 0.5 shard_map.71
  57.9 5.0 %collective-permute-done.16 = bf16[128,768]{1,0:T(8,128)(2,1)S(1)} collective-permute-done((bf16[128,768]{1,0:T(8,128)(2,1)S(1)}, bf16[128,768]{1,0:T(8,128)(2,1)S(1)}, u32[]{:S(2)}, u32[]{:S(2)}) %collective-permute-start.16) | collective-permute-done | bytes 196640 | tf_op jit(solution)/shard_map/ppermute | solution.py:15
  62.9 0.7 %add_convert_fusion = bf16[128,768]{1,0:T(8,128)(2,1)} fusion(f32[128,768]{1,0:T(8,128)S(1)} %shard_map.71, bf16[128,768]{1,0:T(8,128)(2,1)S(1)} %collective-permute-done.16), kind=kLoop, calls=%fused_computation | loop fusion | flops 294912 | bytes 786432 | tf_op jit(solution)/shard_map/convert_element_type | solution.py:185
  (35 shorter events, 0.7 us)
Async XLA Ops:
  0.0 8.9 %copy-start = (s32[12,4,4]{0,2,1:T(4,128)S(1)}, s32[12,4,4]{0,2,1:T(4,128)}, u32[]{:S(2)}) copy-start(s32[12,4,4]{0,2,1:T(4,128)} %param.9) | copy-start | bytes 2308
  0.0 1.0 %copy-start.2 = (bf16[1,128,1536]{2,1,0:T(8,128)(2,1)S(1)}, bf16[1,128,1536]{2,1,0:T(8,128)(2,1)}, u32[]{:S(2)}) copy-start(bf16[1,128,1536]{2,1,0:T(8,128)(2,1)} %param.6) | copy-start | bytes 1179652
  1.0 1.0 %copy-start.3 = (bf16[1,128,1536]{2,1,0:T(8,128)(2,1)S(1)}, bf16[1,128,1536]{2,1,0:T(8,128)(2,1)}, u32[]{:S(2)}) copy-start(bf16[1,128,1536]{2,1,0:T(8,128)(2,1)} %param.7) | copy-start | bytes 1179652
  2.0 1.0 %copy-start.4 = (bf16[1,128,1536]{2,1,0:T(8,128)(2,1)S(1)}, bf16[1,128,1536]{2,1,0:T(8,128)(2,1)}, u32[]{:S(2)}) copy-start(bf16[1,128,1536]{2,1,0:T(8,128)(2,1)} %param.8) | copy-start | bytes 1179652
  3.1 11.5 %collective-permute-start = (bf16[3,128,256]{2,1,0:T(8,128)(2,1)S(1)}, bf16[3,128,256]{2,1,0:T(8,128)(2,1)S(1)}, u32[]{:S(2)}, u32[]{:S(2)}) collective-permute-start(bf16[3,128,256]{2,1,0:T(8,128)(2,1)S(1)} %get-tuple-element.26), channel_id=1, source_target_pairs={{0,4},{4,0},{8,12},{12,8},{1,5},{5,1},{9,13},{13,9},{2,6},{6,2},{1... | collective-permute-start | bytes 589832 | tf_op jit(solution)/shard_map/ppermute | solution.py:15
  6.2 17.1 %collective-permute-start.1 = (bf16[3,128,256]{2,1,0:T(8,128)(2,1)S(1)}, bf16[3,128,256]{2,1,0:T(8,128)(2,1)S(1)}, u32[]{:S(2)}, u32[]{:S(2)}) collective-permute-start(bf16[3,128,256]{2,1,0:T(8,128)(2,1)S(1)} %get-tuple-element.27), channel_id=1, source_target_pairs={{0,8},{4,12},{8,0},{12,4},{1,9},{5,13},{9,1},{13,5},{2,10},{6,14},... | collective-permute-start | bytes 589832 | tf_op jit(solution)/shard_map/ppermute | solution.py:15
  8.8 14.5 %collective-permute-start.2 = (bf16[3,128,256]{2,1,0:T(8,128)(2,1)S(1)}, bf16[3,128,256]{2,1,0:T(8,128)(2,1)S(1)}, u32[]{:S(2)}, u32[]{:S(2)}) collective-permute-start(bf16[3,128,256]{2,1,0:T(8,128)(2,1)S(1)} %get-tuple-element.28), channel_id=1, source_target_pairs={{0,12},{4,8},{8,4},{12,0},{1,13},{5,9},{9,5},{13,1},{2,14},{6,10},... | collective-permute-start | bytes 589832 | tf_op jit(solution)/shard_map/ppermute | solution.py:15
  25.6 5.8 %collective-permute-start.3 = (bf16[4,64,256]{2,1,0:T(8,128)(2,1)S(1)}, bf16[4,64,256]{2,1,0:T(8,128)(2,1)S(1)}, u32[]{:S(2)}, u32[]{:S(2)}) collective-permute-start(bf16[4,64,256]{2,1,0:T(8,128)(2,1)S(1)} %get-tuple-element.30), channel_id=1, source_target_pairs={{0,1},{1,0},{2,3},{3,2},{4,5},{5,4},{6,7},{7,6},{8,9},{9,8},{10,11... | collective-permute-start | bytes 393224 | tf_op jit(solution)/shard_map/ppermute | solution.py:15
  25.7 8.9 %collective-permute-start.10 = (bf16[3,128,128]{2,1,0:T(8,128)(2,1)S(1)}, bf16[3,128,128]{2,1,0:T(8,128)(2,1)S(1)}, u32[]{:S(2)}, u32[]{:S(2)}) collective-permute-start(bf16[3,128,128]{2,1,0:T(8,128)(2,1)S(1)} %get-tuple-element.38), channel_id=1, source_target_pairs={{0,12},{4,8},{8,4},{12,0},{1,13},{5,9},{9,5},{13,1},{2,14},{6,10},... | collective-permute-start | bytes 294920 | tf_op jit(solution)/shard_map/ppermute | solution.py:15
  28.2 7.8 %collective-permute-start.8 = (bf16[3,128,128]{2,1,0:T(8,128)(2,1)S(1)}, bf16[3,128,128]{2,1,0:T(8,128)(2,1)S(1)}, u32[]{:S(2)}, u32[]{:S(2)}) collective-permute-start(bf16[3,128,128]{2,1,0:T(8,128)(2,1)S(1)} %get-tuple-element.36), channel_id=1, source_target_pairs={{0,4},{4,0},{8,12},{12,8},{1,5},{5,1},{9,13},{13,9},{2,6},{6,2},{1... | collective-permute-start | bytes 294920 | tf_op jit(solution)/shard_map/ppermute | solution.py:15
  30.7 9.7 %collective-permute-start.9 = (bf16[3,128,128]{2,1,0:T(8,128)(2,1)S(1)}, bf16[3,128,128]{2,1,0:T(8,128)(2,1)S(1)}, u32[]{:S(2)}, u32[]{:S(2)}) collective-permute-start(bf16[3,128,128]{2,1,0:T(8,128)(2,1)S(1)} %get-tuple-element.37), channel_id=1, source_target_pairs={{0,8},{4,12},{8,0},{12,4},{1,9},{5,13},{9,1},{13,5},{2,10},{6,14},... | collective-permute-start | bytes 294920 | tf_op jit(solution)/shard_map/ppermute | solution.py:15
  31.5 10.2 %collective-permute-start.4 = (bf16[64,256]{1,0:T(8,128)(2,1)S(1)}, bf16[64,256]{1,0:T(8,128)(2,1)S(1)}, u32[]{:S(2)}, u32[]{:S(2)}) collective-permute-start(bf16[64,256]{1,0:T(8,128)(2,1)S(1)} %get-tuple-element.32), channel_id=1, source_target_pairs={{0,4},{4,0},{8,12},{12,8},{1,5},{5,1},{9,13},{13,9},{2,6},{6,2},{1... | collective-permute-start | bytes 98312 | tf_op jit(solution)/shard_map/ppermute | solution.py:15
  33.5 8.3 %collective-permute-start.5 = (bf16[64,256]{1,0:T(8,128)(2,1)S(1)}, bf16[64,256]{1,0:T(8,128)(2,1)S(1)}, u32[]{:S(2)}, u32[]{:S(2)}) collective-permute-start(bf16[64,256]{1,0:T(8,128)(2,1)S(1)} %get-tuple-element.33), channel_id=1, source_target_pairs={{0,8},{4,12},{8,0},{12,4},{1,9},{5,13},{9,1},{13,5},{2,10},{6,14},... | collective-permute-start | bytes 98312 | tf_op jit(solution)/shard_map/ppermute | solution.py:15
  34.6 7.2 %collective-permute-start.6 = (bf16[64,256]{1,0:T(8,128)(2,1)S(1)}, bf16[64,256]{1,0:T(8,128)(2,1)S(1)}, u32[]{:S(2)}, u32[]{:S(2)}) collective-permute-start(bf16[64,256]{1,0:T(8,128)(2,1)S(1)} %get-tuple-element.34), channel_id=1, source_target_pairs={{0,12},{4,8},{8,4},{12,0},{1,13},{5,9},{9,5},{13,1},{2,14},{6,10},... | collective-permute-start | bytes 98312 | tf_op jit(solution)/shard_map/ppermute | solution.py:15
  41.7 1.3 %collective-permute-start.11 = (bf16[4,64,128]{2,1,0:T(8,128)(2,1)S(1)}, bf16[4,64,128]{2,1,0:T(8,128)(2,1)S(1)}, u32[]{:S(2)}, u32[]{:S(2)}) collective-permute-start(bf16[4,64,128]{2,1,0:T(8,128)(2,1)S(1)} %get-tuple-element.40), channel_id=1, source_target_pairs={{0,1},{1,0},{2,3},{3,2},{4,5},{5,4},{6,7},{7,6},{8,9},{9,8},{10,11... | collective-permute-start | bytes 196616 | tf_op jit(solution)/shard_map/ppermute | solution.py:15
  41.8 11.2 %collective-permute-start.7 = (bf16[4,64,256]{2,1,0:T(8,128)(2,1)S(1)}, bf16[4,64,256]{2,1,0:T(8,128)(2,1)S(1)}, u32[]{:S(2)}, u32[]{:S(2)}) collective-permute-start(bf16[4,64,256]{2,1,0:T(8,128)(2,1)S(1)} %shard_map.67.refs_0_), channel_id=1, source_target_pairs={{0,1},{1,0},{2,3},{3,2},{4,5},{5,4},{6,7},{7,6},{8,9},{9,8},{10,11... | collective-permute-start | bytes 393224 | tf_op jit(solution)/shard_map/ppermute | solution.py:15
  43.1 4.5 %collective-permute-start.12 = (bf16[64,128]{1,0:T(8,128)(2,1)S(1)}, bf16[64,128]{1,0:T(8,128)(2,1)S(1)}, u32[]{:S(2)}, u32[]{:S(2)}) collective-permute-start(bf16[64,128]{1,0:T(8,128)(2,1)S(1)} %get-tuple-element.42), channel_id=1, source_target_pairs={{0,4},{4,0},{8,12},{12,8},{1,5},{5,1},{9,13},{13,9},{2,6},{6,2},{1... | collective-permute-start | bytes 49160 | tf_op jit(solution)/shard_map/ppermute | solution.py:15
  43.1 4.7 %collective-permute-start.13 = (bf16[64,128]{1,0:T(8,128)(2,1)S(1)}, bf16[64,128]{1,0:T(8,128)(2,1)S(1)}, u32[]{:S(2)}, u32[]{:S(2)}) collective-permute-start(bf16[64,128]{1,0:T(8,128)(2,1)S(1)} %get-tuple-element.43), channel_id=1, source_target_pairs={{0,8},{4,12},{8,0},{12,4},{1,9},{5,13},{9,1},{13,5},{2,10},{6,14},... | collective-permute-start | bytes 49160 | tf_op jit(solution)/shard_map/ppermute | solution.py:15
  46.2 5.5 %collective-permute-start.14 = (bf16[64,128]{1,0:T(8,128)(2,1)S(1)}, bf16[64,128]{1,0:T(8,128)(2,1)S(1)}, u32[]{:S(2)}, u32[]{:S(2)}) collective-permute-start(bf16[64,128]{1,0:T(8,128)(2,1)S(1)} %get-tuple-element.44), channel_id=1, source_target_pairs={{0,12},{4,8},{8,4},{12,0},{1,13},{5,9},{9,5},{13,1},{2,14},{6,10},... | collective-permute-start | bytes 49160 | tf_op jit(solution)/shard_map/ppermute | solution.py:15
  51.7 1.3 %collective-permute-start.15 = (bf16[4,64,128]{2,1,0:T(8,128)(2,1)S(1)}, bf16[4,64,128]{2,1,0:T(8,128)(2,1)S(1)}, u32[]{:S(2)}, u32[]{:S(2)}) collective-permute-start(bf16[4,64,128]{2,1,0:T(8,128)(2,1)S(1)} %shard_map.70.refs_2_), channel_id=1, source_target_pairs={{0,1},{1,0},{2,3},{3,2},{4,5},{5,4},{6,7},{7,6},{8,9},{9,8},{10,11... | collective-permute-start | bytes 196616 | tf_op jit(solution)/shard_map/ppermute | solution.py:15
  53.0 2.3 %copy-start.1 = (bf16[1536,1536]{1,0:T(8,128)(2,1)S(1)}, bf16[1536,1536]{1,0:T(8,128)(2,1)}, u32[]{:S(2)}) copy-start(bf16[1536,1536]{1,0:T(8,128)(2,1)} %w_ref.3) | copy-start | bytes 14155780
  55.8 7.0 %collective-permute-start.16 = (bf16[128,768]{1,0:T(8,128)(2,1)S(1)}, bf16[128,768]{1,0:T(8,128)(2,1)S(1)}, u32[]{:S(2)}, u32[]{:S(2)}) collective-permute-start(bf16[128,768]{1,0:T(8,128)(2,1)S(1)} %shard_map.72), channel_id=1, source_target_pairs={{0,2},{2,0},{1,3},{3,1},{4,6},{6,4},{5,7},{7,5},{8,10},{10,8},{9,1... | collective-permute-start | bytes 589832 | tf_op jit(solution)/shard_map/ppermute | solution.py:15

commit v2 on v1

--- a/solution.py
+++ b/solution.py
@@ -7,6 +7,7 @@
 from jax.experimental.pallas import tpu as pltpu
 from jax.sharding import PartitionSpec as P
 
+
 HD = 128
 MIB = 1 << 20
 
@@ -15,17 +16,15 @@
     return lax.ppermute(array, axis, [(i, i ^ bits) for i in range(lax.axis_size(axis))])
 
 
-def vmem(count):
-    return [pl.BlockSpec(memory_space=pltpu.VMEM)] * count
-
-
-def call(body, outs, args, flops, limit=16):
+def call(body, outs, args, flops, spaces=None, scratch=(), limit=16):
     moved = sum(a.size * a.dtype.itemsize for a in [*args, *outs])
+    spaces = spaces or [pltpu.VMEM] * len(args)
     return pl.pallas_call(
         body,
         out_shape=outs,
-        in_specs=vmem(len(args)),
-        out_specs=vmem(len(outs)),
+        in_specs=[pl.BlockSpec(memory_space=space) for space in spaces],
+        out_specs=[pl.BlockSpec(memory_space=pltpu.VMEM)] * len(outs),
+        scratch_shapes=scratch,
         compiler_params=pltpu.CompilerParams(vmem_limit_bytes=limit * MIB),
         cost_estimate=pl.CostEstimate(flops=flops, bytes_accessed=moved, transcendentals=0),
     )(*args)
@@ -35,15 +34,52 @@
     return pl.ds(pl.multiple_of(head * HD, HD), count * HD)
 
 
-def pack_body(slots, per, chunks, q_ref, k_ref, v_ref, *outs):
+def start_all(copies, sem):
+    copies = [pltpu.make_async_copy(src, dst, sem.at[i]) for i, (src, dst) in enumerate(copies)]
+    for copy in copies:
+        copy.start()
+    for copy in copies:
+        copy.wait()
+
+
+def pack_body(slots, per, chunks, q_ref, k_ref, v_ref, *refs):
+    outs, sem = refs[:-1], refs[-1]
     place = lax.axis_index("seq")
-    at = 0
-    for first, count in chunks:
+    copies = []
+    for index, (first, count) in enumerate(chunks):
         for slot in range(slots):
             cols = columns((place ^ slot) * per + first, count)
             for part, ref in enumerate((q_ref, k_ref, v_ref)):
-                outs[at][part] = ref[:, cols]
-            at += 1
+                copies.append((ref.at[:, cols], outs[index * slots + slot].at[part]))
+    start_all(copies, sem)
+
+
+def setup_body(slots, per, chunks, w_ref, mask_ref, guidance_ref, *refs):
+    outs, (bias_ref, strength_ref, sem) = refs[:-3], refs[-3:]
+    place, side = lax.axis_index("seq"), lax.axis_index("head")
+    width = outs[0].shape[1]
+    copies = []
+    for index, (first, count) in enumerate(chunks):
+        for mine in range(2):
+            block = 1 - side if mine else side
+            cols = pl.ds(pl.multiple_of(block * width, HD), width)
+            for at in range(slots):
+                src = w_ref.at[pl.ds((at * per + first) * HD, count * HD), cols]
+                copies.append((src, outs[2 * index + mine].at[pl.ds(at * count * HD, count * HD)]))
+    copies = [pltpu.make_async_copy(src, dst, sem.at[i]) for i, (src, dst) in enumerate(copies)]
+    for copy in copies:
+        copy.start()
+    rows = bias_ref.shape[1] // slots
+    for head in range(per):
+        for slot in range(slots):
+            for other in range(slots):
+                listed = mask_ref[place ^ slot, place ^ other, place * per + head]
+                offset = jnp.where((listed > 0) | (slot == other), 0.0, -1e30).astype(jnp.float32)
+                line = head * slots + slot
+                bias_ref[line : line + 1, other * rows : (other + 1) * rows] = jnp.full((1, rows), offset)
+    strength_ref[...] = jnp.full(strength_ref.shape, guidance_ref[0])
+    for copy in copies:
+        copy.wait()
 
 
 def attend_body(slots, first, count, scale, bias_ref, *refs):
@@ -88,38 +124,51 @@
         out[slot] = ins[slot][...]
 
 
-def project_body(slots, per, chunks, mine_side, w_ref, *refs):
-    pairs, (out_ref, wide_ref) = refs[:-2], refs[-2:]
-    place, core, side = lax.axis_index("seq"), lax.axis_index("cfg"), lax.axis_index("head")
-    half = out_ref.shape[0] // 2
-    width = out_ref.shape[1]
-    for index, (first, count) in enumerate(chunks):
-        mine, theirs = pairs[2 * index], pairs[2 * index + 1]
-        for slot in range(slots):
-            cols = columns((place ^ slot) * per + first, count)
-            wide_ref[pl.ds(pl.multiple_of(core * half, half), half), cols] = mine[slot]
-            wide_ref[pl.ds(pl.multiple_of((1 - core) * half, half), half), cols] = theirs[slot]
-    block = side if mine_side else 1 - side
-    weights = w_ref[:, pl.ds(pl.multiple_of(block * width, HD), width)]
-    out_ref[...] = jnp.dot(wide_ref[...], weights, preferred_element_type=jnp.float32).astype(out_ref.dtype)
+def spread(wide_ref, slots, mine_ref, theirs_ref):
+    place, core = lax.axis_index("seq"), lax.axis_index("cfg")
+    half = mine_ref.shape[1]
+    count = mine_ref.shape[2] // HD
+    for slot in range(slots):
+        cols = columns((place ^ slot) * count, count)
+        wide_ref[pl.ds(pl.multiple_of(core * half, half), half), cols] = mine_ref[slot]
+        wide_ref[pl.ds(pl.multiple_of((1 - core) * half, half), half), cols] = theirs_ref[slot]
+
+
+def project_body(slots, w_ref, mine_ref, theirs_ref, out_ref, wide_ref):
+    spread(wide_ref, slots, mine_ref, theirs_ref)
+    out_ref[...] = jnp.dot(
+        wide_ref[...], w_ref[...], preferred_element_type=jnp.float32
+    ).astype(out_ref.dtype)
+
+
+def finish_body(slots, sum_ref, part_ref, w_ref, mine_ref, theirs_ref, w2_ref, mine2_ref, theirs2_ref, out_ref, wide_ref):
+    total = sum_ref[...] + part_ref[...].astype(jnp.float32)
+    for w, mine, theirs in ((w_ref, mine_ref, theirs_ref), (w2_ref, mine2_ref, theirs2_ref)):
+        spread(wide_ref, slots, mine, theirs)
+        total += jnp.dot(wide_ref[...], w[...], preferred_element_type=jnp.float32)
+    out_ref[...] = total.astype(out_ref.dtype)
 
 
 def by_heads(queries, keys, values, band_mask, out_weight, guidance):
     own_q, own_k, own_v = queries[0], keys[0], values[0]
     rows, wide = own_q.shape
     slots = lax.axis_size("seq")
-    place = lax.axis_index("seq")
     per = wide // HD // slots
-    chunks = [(0, per)] if per < 2 else [(0, per - per // 3), (per - per // 3, per // 3)]
-    chunks = [c for c in chunks if c[1] > 0]
+    last = max(1, per // 3)
+    chunks = [(0, per - last), (per - last, last)]
     half = rows // 2
+    width = out_weight.shape[1] // 2
     bf16, f32 = jnp.bfloat16, jnp.float32
+    shape = jax.ShapeDtypeStruct
 
     packed = call(
         functools.partial(pack_body, slots, per, chunks),
-        [jax.ShapeDtypeStruct((3, rows, c * HD), bf16) for _, c in chunks for _ in range(slots)],
+        [shape((3, rows, c * HD), bf16) for _, c in chunks for _ in range(slots)],
         [own_q, own_k, own_v],
         0,
+        spaces=[pltpu.HBM] * 3,
+        scratch=[pltpu.SemaphoreType.DMA((3 * slots * len(chunks),))],
+        limit=53,
     )
     order = sorted(range(1, slots), reverse=True)
     received = []
@@ -129,30 +178,31 @@
             got[slot] = swapped(packed[index * slots + slot], "seq", slot)
         received.append([got[s] for s in range(slots)])
 
-    tiles = jnp.arange(slots)
-    mine = lax.dynamic_slice_in_dim(band_mask, place * per, per, 0)
-    pick = ((place ^ tiles)[:, None] == tiles[None, :])[None, :, None, :, None] & (
-        ((place ^ tiles)[:, None] == tiles[None, :])[None, None, :, None, :]
-    )
-    listed = jnp.sum(jnp.where(pick, mine[:, None, None], 0), axis=(3, 4))
-    allowed = (listed + jnp.eye(slots, dtype=jnp.int32)[None]) > 0
-    bias = jnp.where(allowed, 0.0, -1e30).astype(f32)
-    bias = jnp.repeat(bias.reshape(per * slots, slots), own_k.shape[0], axis=1)
-    strength = jnp.broadcast_to(guidance.reshape(1, 1), (8, HD))
+    *weights, bias, strength = call(
+        functools.partial(setup_body, slots, per, chunks),
+        [shape((slots * c * HD, width), bf16) for _, c in chunks for _ in range(2)]
+        + [shape((per * slots, slots * rows), f32), shape((8, HD), f32)],
+        [out_weight, jnp.transpose(band_mask, (1, 2, 0)), guidance],
+        10**9,
+        spaces=[pltpu.HBM, pltpu.SMEM, pltpu.SMEM],
+        scratch=[pltpu.SemaphoreType.DMA((2 * slots * len(chunks),))],
+    )
+    keep0, send0, keep1, send1 = weights
+    other1 = swapped(send1, "head", 1)
 
     shared = []
     for (first, count), blocks in zip(chunks, received):
-        shape = jax.ShapeDtypeStruct((slots, half, count * HD), bf16)
+        block = shape((slots, half, count * HD), bf16)
         keep, send = call(
             functools.partial(attend_body, slots, first, count, HD ** (-0.5)),
-            [shape, shape],
+            [block, block],
             [bias, *blocks],
             4 * count * (slots * rows) ** 2 * HD,
         )
         other = swapped(send, "cfg", 1)
         guided = call(
             functools.partial(guide_body, slots),
-            [jax.ShapeDtypeStruct((half, count * HD), bf16)] * slots,
+            [shape((half, count * HD), bf16)] * slots,
             [strength, keep, other],
             8 * slots * half * count * HD,
         )
@@ -160,29 +210,36 @@
         for slot in order:
             back[slot] = swapped(guided[slot], "seq", slot)
         (mine,) = call(
-            functools.partial(join_body, slots), [shape], [back[s] for s in range(slots)], 0
+            functools.partial(join_body, slots), [block],
+            [back[s] for s in range(slots)], 0,
         )
-        shared += [mine, swapped(mine, "cfg", 1)]
-
-    width = out_weight.shape[1] // 2
-
-    def project(mine_side, dtype):
-        return pl.pallas_call(
-            functools.partial(project_body, slots, per, chunks, mine_side),
-            out_shape=jax.ShapeDtypeStruct((rows, width), dtype),
-            in_specs=vmem(1 + len(shared)),
-            out_specs=vmem(1)[0],
-            scratch_shapes=[pltpu.VMEM((rows, wide), bf16)],
-            compiler_params=pltpu.CompilerParams(vmem_limit_bytes=16 * MIB),
-            cost_estimate=pl.CostEstimate(
-                flops=2 * rows * wide * width,
-                bytes_accessed=wide * width * 2,
-                transcendentals=0,
-            ),
-        )(out_weight, *shared)
-
-    theirs = swapped(project(False, bf16), "head", 1)
-    return (project(True, f32) + theirs.astype(f32)).astype(bf16)
+        shared.append((mine, swapped(mine, "cfg", 1)))
+    (mine0, theirs0), (mine1, theirs1) = shared
+
+    def project(weight, dtype):
+        depth = weight.shape[0]
+        (out,) = call(
+            functools.partial(project_body, slots),
+            [shape((rows, width), dtype)],
+            [weight, mine0, theirs0],
+            2 * rows * depth * width,
+            scratch=[pltpu.VMEM((rows, depth), bf16)],
+        )
+        return out
+
+    part = swapped(project(send0, bf16), "head", 1)
+    total = project(keep0, f32)
+    mine2 = swapped(mine1, "head", 1)
+    theirs2 = swapped(mine2, "cfg", 1)
+    depth = keep1.shape[0]
+    (out,) = call(
+        functools.partial(finish_body, slots),
+        [shape((rows, width), bf16)],
+        [total, part, keep1, mine1, theirs1, other1, mine2, theirs2],
+        4 * rows * depth * width,
+        scratch=[pltpu.VMEM((rows, depth), bf16)],
+    )
+    return out
 
 
 def by_bands(queries, keys, values, band_mask, out_weight, guidance):
@@ -233,10 +290,11 @@
     slots = lax.axis_size("seq")
     heads = queries.shape[2] // HD
     rows = queries.shape[1]
-    fits = heads % slots == 0 and slots & (slots - 1) == 0 and rows == keys.shape[1]
+    fits = heads % slots == 0 and heads // slots > 1 and slots & (slots - 1) == 0 and rows == keys.shape[1]
     fits = fits and rows % 32 == 0 and lax.axis_size("cfg") == 2 and lax.axis_size("head") == 2
-    plan = by_heads if fits else by_bands
-    return plan(queries, keys, values, band_mask, out_weight, guidance)
+    if not fits:
+        return by_bands(queries, keys, values, band_mask, out_weight, guidance)
+    return by_heads(queries, keys, values, band_mask, out_weight, guidance)
 
 
 def solution(mesh):

time: 63.8 us -> 71.5 us (1.12)
  waiting for transfers between devices: 28.6 us -> 35.4 us
  Pallas kernels: 4.76 us -> 8.83 us
  local copies, waits for them, and re-layouts: 5.63 us -> 3.03 us
  other arithmetic: 1.83 us -> 0 us
  starting transfers between devices: 21.9 us -> 23.2 us
    ppermute x17 -> x20, waiting for transfers between devices: 28.6 us -> 35.4 us  [swapped(): lax.ppermute(array, axis, [(i, i ^ bits) for i in range(lax.axis_size(axi...]
    pallas_call x9 -> x11, Pallas kernels: 4.76 us -> 8.83 us  [call(): pl.pallas_call(body, out_shape=outs, in_specs=[pl.BlockSpec(memory_space=...]
    unnamed x12 -> x4, local copies, waits for them, and re-layouts: 5.36 us -> 3.03 us
    ppermute x17 -> x20, starting transfers between devices: 21.9 us -> 23.2 us  [swapped(): lax.ppermute(array, axis, [(i, i ^ bits) for i in range(lax.axis_size(axi...]
    reduce_sum x1 -> x0, other arithmetic: 0.95 us -> none  [by_heads(): listed = jnp.sum(jnp.where(pick, mine[:, None, None], 0), axis=(3, 4))]
    convert_element_type x2 -> x0, other arithmetic: 0.72 us -> none  [the longest x1 0.71 us: by_heads(): return (project(True, f32) + theirs.astype(f32)).astype(bf16)]
  transfers between devices with their start and end apart: 17 -> 20, of which waited for: 8 -> 12; matrix products, arithmetic and copies ran while one was open for 2% -> 0% of each run, Pallas kernels for 3% -> 9%
where the time goes in v2:
time: 71.5 us; the launch traced here: 71.2 us
  waiting for transfers between devices  35.4 us (50%)
  starting transfers between devices  23.2 us (32%)
  Pallas kernels  8.83 us (12%)
  local copies, waits for them, and re-layouts  3.03 us (4%)
  between operations  0.78 us (1%)
    ppermute x20, waiting for transfers between devices, swapped(): lax.ppermute(array, axis, [(i, i ^ bits) for i in range(lax.axis_size(axi...  35.4 us
    ppermute x20, starting transfers between devices, swapped(): lax.ppermute(array, axis, [(i, i ^ bits) for i in range(lax.axis_size(axi...  23.2 us
    pallas_call x11, Pallas kernels, call(): pl.pallas_call(body, out_shape=outs, in_specs=[pl.BlockSpec(memory_space=...  8.83 us
    unnamed x4, local copies, waits for them, and re-layouts  3.03 us
  transfers between devices with their start and end apart: 20, of which 12 were waited for; matrix products, arithmetic and copies ran while one was open for 0% of the time, Pallas kernels for 9%

profile of v2, /device:TPU:0, one launch (start us, length us, event | category | flops | bytes accessed | tf_op | source)
XLA Modules:
  0.0 71.2 jit_solution(3480417757552487064)
XLA Ops:
  0.7 2.3 %copy-done = bf16[1536,1536]{1,0:T(8,128)(2,1)S(1)} copy-done((bf16[1536,1536]{1,0:T(8,128)(2,1)S(1)}, bf16[1536,1536]{1,0:T(8,128)(2,1)}, u32[]{:S(2)}) %copy-start) | copy-done | bytes 4718616
  3.0 0.7 copy-done.1
  3.7 1.3 %shard_map.64 = (bf16[1024,768]{1,0:T(8,128)(2,1)S(1)}, bf16[1024,768]{1,0:T(8,128)(2,1)S(1)}, bf16[512,768]{1,0:T(8,128)(2,1)S(1)}, bf16[512,768]{1,0:T(8,128)(...) custom-call(bf16[1536,1536]{1,0:T(8,128)(2,1)S(1)} %copy-done, s32[4,4,12]{2,1,0:T(4,128)S(1)} %bitcast.4, ...), custom_call_target="tpu_custom_call" | custom-call | flops 1000000000 | bytes 9466628 | tf_op jit(solution)/shard_map/pallas_call | solution.py:22
  5.0 3.0 %collective-permute-start.17 = (bf16[512,768]{1,0:T(8,128)(2,1)S(1)}, bf16[512,768]{1,0:T(8,128)(2,1)S(1)}, u32[]{:S(2)}, u32[]{:S(2)}) collective-permute-start(bf16[512,768]{1,0:T(8,128)(2,1)S(1)} %get-tuple-element.56), channel_id=1, source_target_pairs={{0,2},{2,0},{1,3},{3,1},{4,6},{6,4},{5,7},{7,5},{8,10},{10,8},{9,1... | collective-permute-start | bytes 2359304 | tf_op jit(solution)/shard_map/ppermute | solution.py:16
  8.0 2.1 %shard_map.65 = (bf16[3,128,256]{2,1,0:T(8,128)(2,1)S(1)}, bf16[3,128,256]{2,1,0:T(8,128)(2,1)S(1)}, bf16[3,128,256]{2,1,0:T(8,128)(2,1)S(1)}, bf16[3,128,256]{2...) custom-call(bf16[128,1536]{1,0:T(8,128)(2,1)} %bitcast.5, ...), custom_call_target="tpu_custom_call" | custom-call | bytes 2359296 | tf_op jit(solution)/shard_map/pallas_call | solution.py:22
  10.1 1.6 %collective-permute-start = (bf16[3,128,256]{2,1,0:T(8,128)(2,1)S(1)}, bf16[3,128,256]{2,1,0:T(8,128)(2,1)S(1)}, u32[]{:S(2)}, u32[]{:S(2)}) collective-permute-start(bf16[3,128,256]{2,1,0:T(8,128)(2,1)S(1)} %get-tuple-element.35), channel_id=1, source_target_pairs={{0,4},{4,0},{8,12},{12,8},{1,5},{5,1},{9,13},{13,9},{2,6},{6,2},{1... | collective-permute-start | bytes 589832 | tf_op jit(solution)/shard_map/ppermute | solution.py:16
  11.8 2.6 %collective-permute-start.1 = (bf16[3,128,256]{2,1,0:T(8,128)(2,1)S(1)}, bf16[3,128,256]{2,1,0:T(8,128)(2,1)S(1)}, u32[]{:S(2)}, u32[]{:S(2)}) collective-permute-start(bf16[3,128,256]{2,1,0:T(8,128)(2,1)S(1)} %get-tuple-element.36), channel_id=1, source_target_pairs={{0,8},{4,12},{8,0},{12,4},{1,9},{5,13},{9,1},{13,5},{2,10},{6,14},... | collective-permute-start | bytes 589832 | tf_op jit(solution)/shard_map/ppermute | solution.py:16
  14.6 5.2 %collective-permute-done.refs_1_ = bf16[3,128,256]{2,1,0:T(8,128)(2,1)S(1)} collective-permute-done((bf16[3,128,256]{2,1,0:T(8,128)(2,1)S(1)}, bf16[3,128,256]{2,1,0:T(8,128)(2,1)S(1)}, u32[]{:S(2)}, u32[]{:S(2)}) %collective-permute-start) | collective-permute-done | bytes 196640 | tf_op jit(solution)/shard_map/ppermute | solution.py:16
  19.8 9.1 %collective-permute-done.1.refs_2_ = bf16[3,128,256]{2,1,0:T(8,128)(2,1)S(1)} collective-permute-done((bf16[3,128,256]{2,1,0:T(8,128)(2,1)S(1)}, bf16[3,128,256]{2,1,0:T(8,128)(2,1)S(1)}, u32[]{:S(2)}, u32[]{:S(2)}) %collective-permute-start.1) | collective-permute-done | bytes 196640 | tf_op jit(solution)/shard_map/ppermute | solution.py:16
  28.9 2.2 %shard_map.66 = (bf16[4,64,256]{2,1,0:T(8,128)(2,1)S(1)}, bf16[4,64,256]{2,1,0:T(8,128)(2,1)S(1)}) custom-call(f32[12,512]{1,0:T(8,128)S(1)} %get-tuple-element.33.bias_ref, bf16[3,128,256]{2,1,0:T(8,128)(2,1)S(1)} %get-tuple-element.34.refs_0_, bf16[3,128,256]{2,1,0:T(8,128)(2,1)S(1)} %collective-permute-done.refs_1_, ...), custom_call_target="tpu_custom_call" | custom-call | flops 268435456 | bytes 1073152 | tf_op jit(solution)/shard_map/pallas_call | solution.py:22
  31.2 1.3 %collective-permute-done.3.other_ref = bf16[4,64,256]{2,1,0:T(8,128)(2,1)S(1)} collective-permute-done((bf16[4,64,256]{2,1,0:T(8,128)(2,1)S(1)}, bf16[4,64,256]{2,1,0:T(8,128)(2,1)S(1)}, u32[]{:S(2)}, u32[]{:S(2)}) %collective-permute-start.3) | collective-permute-done | bytes 131104 | tf_op jit(solution)/shard_map/ppermute | solution.py:16
  32.6 3.2 %collective-permute-start.4 = (bf16[64,256]{1,0:T(8,128)(2,1)S(1)}, bf16[64,256]{1,0:T(8,128)(2,1)S(1)}, u32[]{:S(2)}, u32[]{:S(2)}) collective-permute-start(bf16[64,256]{1,0:T(8,128)(2,1)S(1)} %get-tuple-element.41), channel_id=1, source_target_pairs={{0,4},{4,0},{8,12},{12,8},{1,5},{5,1},{9,13},{13,9},{2,6},{6,2},{1... | collective-permute-start | bytes 98312 | tf_op jit(solution)/shard_map/ppermute | solution.py:16
  35.8 1.1 %collective-permute-start.5 = (bf16[64,256]{1,0:T(8,128)(2,1)S(1)}, bf16[64,256]{1,0:T(8,128)(2,1)S(1)}, u32[]{:S(2)}, u32[]{:S(2)}) collective-permute-start(bf16[64,256]{1,0:T(8,128)(2,1)S(1)} %get-tuple-element.42), channel_id=1, source_target_pairs={{0,8},{4,12},{8,0},{12,4},{1,9},{5,13},{9,1},{13,5},{2,10},{6,14},... | collective-permute-start | bytes 98312 | tf_op jit(solution)/shard_map/ppermute | solution.py:16
  36.9 1.4 %collective-permute-start.6 = (bf16[64,256]{1,0:T(8,128)(2,1)S(1)}, bf16[64,256]{1,0:T(8,128)(2,1)S(1)}, u32[]{:S(2)}, u32[]{:S(2)}) collective-permute-start(bf16[64,256]{1,0:T(8,128)(2,1)S(1)} %get-tuple-element.43), channel_id=1, source_target_pairs={{0,12},{4,8},{8,4},{12,0},{1,13},{5,9},{9,5},{13,1},{2,14},{6,10},... | collective-permute-start | bytes 98312 | tf_op jit(solution)/shard_map/ppermute | solution.py:16
  38.3 2.9 %collective-permute-done.5.refs_2_ = bf16[64,256]{1,0:T(8,128)(2,1)S(1)} collective-permute-done((bf16[64,256]{1,0:T(8,128)(2,1)S(1)}, bf16[64,256]{1,0:T(8,128)(2,1)S(1)}, u32[]{:S(2)}, u32[]{:S(2)}) %collective-permute-start.5) | collective-permute-done | bytes 32800 | tf_op jit(solution)/shard_map/ppermute | solution.py:16
  41.2 1.4 %collective-permute-done.6.refs_3_ = bf16[64,256]{1,0:T(8,128)(2,1)S(1)} collective-permute-done((bf16[64,256]{1,0:T(8,128)(2,1)S(1)}, bf16[64,256]{1,0:T(8,128)(2,1)S(1)}, u32[]{:S(2)}, u32[]{:S(2)}) %collective-permute-start.6) | collective-permute-done | bytes 32800 | tf_op jit(solution)/shard_map/ppermute | solution.py:16
  42.7 0.9 %collective-permute-start.10 = (bf16[3,128,128]{2,1,0:T(8,128)(2,1)S(1)}, bf16[3,128,128]{2,1,0:T(8,128)(2,1)S(1)}, u32[]{:S(2)}, u32[]{:S(2)}) collective-permute-start(bf16[3,128,128]{2,1,0:T(8,128)(2,1)S(1)} %get-tuple-element.48), channel_id=1, source_target_pairs={{0,8},{4,12},{8,0},{12,4},{1,9},{5,13},{9,1},{13,5},{2,10},{6,14},... | collective-permute-start | bytes 294920 | tf_op jit(solution)/shard_map/ppermute | solution.py:16
  43.6 1.7 %collective-permute-start.11 = (bf16[3,128,128]{2,1,0:T(8,128)(2,1)S(1)}, bf16[3,128,128]{2,1,0:T(8,128)(2,1)S(1)}, u32[]{:S(2)}, u32[]{:S(2)}) collective-permute-start(bf16[3,128,128]{2,1,0:T(8,128)(2,1)S(1)} %get-tuple-element.49), channel_id=1, source_target_pairs={{0,12},{4,8},{8,4},{12,0},{1,13},{5,9},{9,5},{13,1},{2,14},{6,10},... | collective-permute-start | bytes 294920 | tf_op jit(solution)/shard_map/ppermute | solution.py:16
  45.3 1.0 %collective-permute-start.9 = (bf16[3,128,128]{2,1,0:T(8,128)(2,1)S(1)}, bf16[3,128,128]{2,1,0:T(8,128)(2,1)S(1)}, u32[]{:S(2)}, u32[]{:S(2)}) collective-permute-start(bf16[3,128,128]{2,1,0:T(8,128)(2,1)S(1)} %get-tuple-element.47), channel_id=1, source_target_pairs={{0,4},{4,0},{8,12},{12,8},{1,5},{5,1},{9,13},{13,9},{2,6},{6,2},{1... | collective-permute-start | bytes 294920 | tf_op jit(solution)/shard_map/ppermute | solution.py:16
  46.3 6.4 %collective-permute-done.10.refs_2_ = bf16[3,128,128]{2,1,0:T(8,128)(2,1)S(1)} collective-permute-done((bf16[3,128,128]{2,1,0:T(8,128)(2,1)S(1)}, bf16[3,128,128]{2,1,0:T(8,128)(2,1)S(1)}, u32[]{:S(2)}, u32[]{:S(2)}) %collective-permute-start.10) | collective-permute-done | bytes 98336 | tf_op jit(solution)/shard_map/ppermute | solution.py:16
  52.7 1.3 %collective-permute-done.9.refs_1_ = bf16[3,128,128]{2,1,0:T(8,128)(2,1)S(1)} collective-permute-done((bf16[3,128,128]{2,1,0:T(8,128)(2,1)S(1)}, bf16[3,128,128]{2,1,0:T(8,128)(2,1)S(1)}, u32[]{:S(2)}, u32[]{:S(2)}) %collective-permute-start.9) | collective-permute-done | bytes 98336 | tf_op jit(solution)/shard_map/ppermute | solution.py:16
  54.0 1.2 %shard_map.71 = (bf16[4,64,128]{2,1,0:T(8,128)(2,1)S(1)}, bf16[4,64,128]{2,1,0:T(8,128)(2,1)S(1)}) custom-call(f32[12,512]{1,0:T(8,128)S(1)} %get-tuple-element.33.bias_ref, bf16[3,128,128]{2,1,0:T(8,128)(2,1)S(1)} %get-tuple-element.46.refs_0_, bf16[3,128,128]{2,1,0:T(8,128)(2,1)S(1)} %collective-permute-done.9.refs_1_, ...), custom_call_target="tpu_custom_call" | custom-call | flops 134217728 | bytes 548864 | tf_op jit(solution)/shard_map/pallas_call | solution.py:22
  55.7 0.6 collective-permute-start.8
  56.6 1.4 %collective-permute-start.13 = (bf16[64,128]{1,0:T(8,128)(2,1)S(1)}, bf16[64,128]{1,0:T(8,128)(2,1)S(1)}, u32[]{:S(2)}, u32[]{:S(2)}) collective-permute-start(bf16[64,128]{1,0:T(8,128)(2,1)S(1)} %get-tuple-element.53), channel_id=1, source_target_pairs={{0,4},{4,0},{8,12},{12,8},{1,5},{5,1},{9,13},{13,9},{2,6},{6,2},{1... | collective-permute-start | bytes 49160 | tf_op jit(solution)/shard_map/ppermute | solution.py:16
  58.0 1.1 %collective-permute-start.14 = (bf16[64,128]{1,0:T(8,128)(2,1)S(1)}, bf16[64,128]{1,0:T(8,128)(2,1)S(1)}, u32[]{:S(2)}, u32[]{:S(2)}) collective-permute-start(bf16[64,128]{1,0:T(8,128)(2,1)S(1)} %get-tuple-element.54), channel_id=1, source_target_pairs={{0,8},{4,12},{8,0},{12,4},{1,9},{5,13},{9,1},{13,5},{2,10},{6,14},... | collective-permute-start | bytes 49160 | tf_op jit(solution)/shard_map/ppermute | solution.py:16
  59.1 1.9 %collective-permute-start.15 = (bf16[64,128]{1,0:T(8,128)(2,1)S(1)}, bf16[64,128]{1,0:T(8,128)(2,1)S(1)}, u32[]{:S(2)}, u32[]{:S(2)}) collective-permute-start(bf16[64,128]{1,0:T(8,128)(2,1)S(1)} %get-tuple-element.55), channel_id=1, source_target_pairs={{0,12},{4,8},{8,4},{12,0},{1,13},{5,9},{9,5},{13,1},{2,14},{6,10},... | collective-permute-start | bytes 49160 | tf_op jit(solution)/shard_map/ppermute | solution.py:16
  61.0 1.6 %collective-permute-done.14.refs_2_ = bf16[64,128]{1,0:T(8,128)(2,1)S(1)} collective-permute-done((bf16[64,128]{1,0:T(8,128)(2,1)S(1)}, bf16[64,128]{1,0:T(8,128)(2,1)S(1)}, u32[]{:S(2)}, u32[]{:S(2)}) %collective-permute-start.14) | collective-permute-done | bytes 16416 | tf_op jit(solution)/shard_map/ppermute | solution.py:16
  62.6 2.0 %collective-permute-done.15.refs_3_ = bf16[64,128]{1,0:T(8,128)(2,1)S(1)} collective-permute-done((bf16[64,128]{1,0:T(8,128)(2,1)S(1)}, bf16[64,128]{1,0:T(8,128)(2,1)S(1)}, u32[]{:S(2)}, u32[]{:S(2)}) %collective-permute-start.15) | collective-permute-done | bytes 16416 | tf_op jit(solution)/shard_map/ppermute | solution.py:16
  64.6 1.3 %collective-permute-start.18 = (bf16[4,64,128]{2,1,0:T(8,128)(2,1)S(1)}, bf16[4,64,128]{2,1,0:T(8,128)(2,1)S(1)}, u32[]{:S(2)}, u32[]{:S(2)}) collective-permute-start(bf16[4,64,128]{2,1,0:T(8,128)(2,1)S(1)} %shard_map.73.mine_ref), channel_id=1, source_target_pairs={{0,2},{2,0},{1,3},{3,1},{4,6},{6,4},{5,7},{7,5},{8,10},{10,8},{9,1... | collective-permute-start | bytes 196616 | tf_op jit(solution)/shard_map/ppermute | solution.py:16
  65.9 3.0 %collective-permute-done.18.mine2_ref = bf16[4,64,128]{2,1,0:T(8,128)(2,1)S(1)} collective-permute-done((bf16[4,64,128]{2,1,0:T(8,128)(2,1)S(1)}, bf16[4,64,128]{2,1,0:T(8,128)(2,1)S(1)}, u32[]{:S(2)}, u32[]{:S(2)}) %collective-permute-start.18) | collective-permute-done | bytes 65568 | tf_op jit(solution)/shard_map/ppermute | solution.py:16
  69.3 0.8 %collective-permute-done.19.theirs2_ref = bf16[4,64,128]{2,1,0:T(8,128)(2,1)S(1)} collective-permute-done((bf16[4,64,128]{2,1,0:T(8,128)(2,1)S(1)}, bf16[4,64,128]{2,1,0:T(8,128)(2,1)S(1)}, u32[]{:S(2)}, u32[]{:S(2)}) %collective-permute-start.19) | collective-permute-done | bytes 65568 | tf_op jit(solution)/shard_map/ppermute | solution.py:16
  70.2 1.1 %shard_map.74 = bf16[128,768]{1,0:T(8,128)(2,1)} custom-call(f32[128,768]{1,0:T(8,128)S(1)} %shard_map.69.sum_ref, bf16[128,768]{1,0:T(8,128)(2,1)S(1)} %collective-permute-done.8.part_ref, bf16[512,768]{1,0:T(8,128)(2,1)S(1)} %get-tuple-element.45.w_ref, bf16[4,64,128]{2,1,0:T(8,128)(2,1)S(1)} %shard_map.73.mine_ref, ...), custom_call_target="tpu_custom_call" | custom-call | flops 201326592 | bytes 2621440 | tf_op jit(solution)/shard_map/pallas_call | solution.py:22
  (23 shorter events, 1.6 us)
Async XLA Ops:
  0.7 2.3 %copy-start = (bf16[1536,1536]{1,0:T(8,128)(2,1)S(1)}, bf16[1536,1536]{1,0:T(8,128)(2,1)}, u32[]{:S(2)}) copy-start(bf16[1536,1536]{1,0:T(8,128)(2,1)} %w_ref.1) | copy-start | bytes 14155780
  3.0 0.7 copy-start.1
  5.0 65.2 %collective-permute-start.17 = (bf16[512,768]{1,0:T(8,128)(2,1)S(1)}, bf16[512,768]{1,0:T(8,128)(2,1)S(1)}, u32[]{:S(2)}, u32[]{:S(2)}) collective-permute-start(bf16[512,768]{1,0:T(8,128)(2,1)S(1)} %get-tuple-element.56), channel_id=1, source_target_pairs={{0,2},{2,0},{1,3},{3,1},{4,6},{6,4},{5,7},{7,5},{8,10},{10,8},{9,1... | collective-permute-start | bytes 2359304 | tf_op jit(solution)/shard_map/ppermute | solution.py:16
  10.1 9.7 %collective-permute-start = (bf16[3,128,256]{2,1,0:T(8,128)(2,1)S(1)}, bf16[3,128,256]{2,1,0:T(8,128)(2,1)S(1)}, u32[]{:S(2)}, u32[]{:S(2)}) collective-permute-start(bf16[3,128,256]{2,1,0:T(8,128)(2,1)S(1)} %get-tuple-element.35), channel_id=1, source_target_pairs={{0,4},{4,0},{8,12},{12,8},{1,5},{5,1},{9,13},{13,9},{2,6},{6,2},{1... | collective-permute-start | bytes 589832 | tf_op jit(solution)/shard_map/ppermute | solution.py:16
  11.8 17.1 %collective-permute-start.1 = (bf16[3,128,256]{2,1,0:T(8,128)(2,1)S(1)}, bf16[3,128,256]{2,1,0:T(8,128)(2,1)S(1)}, u32[]{:S(2)}, u32[]{:S(2)}) collective-permute-start(bf16[3,128,256]{2,1,0:T(8,128)(2,1)S(1)} %get-tuple-element.36), channel_id=1, source_target_pairs={{0,8},{4,12},{8,0},{12,4},{1,9},{5,13},{9,1},{13,5},{2,10},{6,14},... | collective-permute-start | bytes 589832 | tf_op jit(solution)/shard_map/ppermute | solution.py:16
  14.4 14.5 %collective-permute-start.2 = (bf16[3,128,256]{2,1,0:T(8,128)(2,1)}, bf16[3,128,256]{2,1,0:T(8,128)(2,1)S(1)}, u32[]{:S(2)}, u32[]{:S(2)}) collective-permute-start(bf16[3,128,256]{2,1,0:T(8,128)(2,1)} %get-tuple-element.37), channel_id=1, source_target_pairs={{0,12},{4,8},{8,4},{12,0},{1,13},{5,9},{9,5},{13,1},{2,14},{6,10},... | collective-permute-start | bytes 589832 | tf_op jit(solution)/shard_map/ppermute | solution.py:16
  31.1 1.4 %collective-permute-start.3 = (bf16[4,64,256]{2,1,0:T(8,128)(2,1)S(1)}, bf16[4,64,256]{2,1,0:T(8,128)(2,1)S(1)}, u32[]{:S(2)}, u32[]{:S(2)}) collective-permute-start(bf16[4,64,256]{2,1,0:T(8,128)(2,1)S(1)} %get-tuple-element.39), channel_id=1, source_target_pairs={{0,1},{1,0},{2,3},{3,2},{4,5},{5,4},{6,7},{7,6},{8,9},{9,8},{10,11... | collective-permute-start | bytes 393224 | tf_op jit(solution)/shard_map/ppermute | solution.py:16
  32.6 5.7 %collective-permute-start.4 = (bf16[64,256]{1,0:T(8,128)(2,1)S(1)}, bf16[64,256]{1,0:T(8,128)(2,1)S(1)}, u32[]{:S(2)}, u32[]{:S(2)}) collective-permute-start(bf16[64,256]{1,0:T(8,128)(2,1)S(1)} %get-tuple-element.41), channel_id=1, source_target_pairs={{0,4},{4,0},{8,12},{12,8},{1,5},{5,1},{9,13},{13,9},{2,6},{6,2},{1... | collective-permute-start | bytes 98312 | tf_op jit(solution)/shard_map/ppermute | solution.py:16
  35.8 5.4 %collective-permute-start.5 = (bf16[64,256]{1,0:T(8,128)(2,1)S(1)}, bf16[64,256]{1,0:T(8,128)(2,1)S(1)}, u32[]{:S(2)}, u32[]{:S(2)}) collective-permute-start(bf16[64,256]{1,0:T(8,128)(2,1)S(1)} %get-tuple-element.42), channel_id=1, source_target_pairs={{0,8},{4,12},{8,0},{12,4},{1,9},{5,13},{9,1},{13,5},{2,10},{6,14},... | collective-permute-start | bytes 98312 | tf_op jit(solution)/shard_map/ppermute | solution.py:16
  36.9 5.7 %collective-permute-start.6 = (bf16[64,256]{1,0:T(8,128)(2,1)S(1)}, bf16[64,256]{1,0:T(8,128)(2,1)S(1)}, u32[]{:S(2)}, u32[]{:S(2)}) collective-permute-start(bf16[64,256]{1,0:T(8,128)(2,1)S(1)} %get-tuple-element.43), channel_id=1, source_target_pairs={{0,12},{4,8},{8,4},{12,0},{1,13},{5,9},{9,5},{13,1},{2,14},{6,10},... | collective-permute-start | bytes 98312 | tf_op jit(solution)/shard_map/ppermute | solution.py:16
  42.6 12.6 %collective-permute-start.7 = (bf16[4,64,256]{2,1,0:T(8,128)(2,1)S(1)}, bf16[4,64,256]{2,1,0:T(8,128)(2,1)S(1)}, u32[]{:S(2)}, u32[]{:S(2)}) collective-permute-start(bf16[4,64,256]{2,1,0:T(8,128)(2,1)S(1)} %shard_map.68.mine_ref), channel_id=1, source_target_pairs={{0,1},{1,0},{2,3},{3,2},{4,5},{5,4},{6,7},{7,6},{8,9},{9,8},{10,11... | collective-permute-start | bytes 393224 | tf_op jit(solution)/shard_map/ppermute | solution.py:16
  42.7 10.0 %collective-permute-start.10 = (bf16[3,128,128]{2,1,0:T(8,128)(2,1)S(1)}, bf16[3,128,128]{2,1,0:T(8,128)(2,1)S(1)}, u32[]{:S(2)}, u32[]{:S(2)}) collective-permute-start(bf16[3,128,128]{2,1,0:T(8,128)(2,1)S(1)} %get-tuple-element.48), channel_id=1, source_target_pairs={{0,8},{4,12},{8,0},{12,4},{1,9},{5,13},{9,1},{13,5},{2,10},{6,14},... | collective-permute-start | bytes 294920 | tf_op jit(solution)/shard_map/ppermute | solution.py:16
  43.6 9.1 %collective-permute-start.11 = (bf16[3,128,128]{2,1,0:T(8,128)(2,1)S(1)}, bf16[3,128,128]{2,1,0:T(8,128)(2,1)S(1)}, u32[]{:S(2)}, u32[]{:S(2)}) collective-permute-start(bf16[3,128,128]{2,1,0:T(8,128)(2,1)S(1)} %get-tuple-element.49), channel_id=1, source_target_pairs={{0,12},{4,8},{8,4},{12,0},{1,13},{5,9},{9,5},{13,1},{2,14},{6,10},... | collective-permute-start | bytes 294920 | tf_op jit(solution)/shard_map/ppermute | solution.py:16
  45.3 8.7 %collective-permute-start.9 = (bf16[3,128,128]{2,1,0:T(8,128)(2,1)S(1)}, bf16[3,128,128]{2,1,0:T(8,128)(2,1)S(1)}, u32[]{:S(2)}, u32[]{:S(2)}) collective-permute-start(bf16[3,128,128]{2,1,0:T(8,128)(2,1)S(1)} %get-tuple-element.47), channel_id=1, source_target_pairs={{0,4},{4,0},{8,12},{12,8},{1,5},{5,1},{9,13},{13,9},{2,6},{6,2},{1... | collective-permute-start | bytes 294920 | tf_op jit(solution)/shard_map/ppermute | solution.py:16
  55.2 1.3 %collective-permute-start.12 = (bf16[4,64,128]{2,1,0:T(8,128)(2,1)S(1)}, bf16[4,64,128]{2,1,0:T(8,128)(2,1)S(1)}, u32[]{:S(2)}, u32[]{:S(2)}) collective-permute-start(bf16[4,64,128]{2,1,0:T(8,128)(2,1)S(1)} %get-tuple-element.51), channel_id=1, source_target_pairs={{0,1},{1,0},{2,3},{3,2},{4,5},{5,4},{6,7},{7,6},{8,9},{9,8},{10,11... | collective-permute-start | bytes 196616 | tf_op jit(solution)/shard_map/ppermute | solution.py:16
  55.7 14.5 %collective-permute-start.8 = (bf16[128,768]{1,0:T(8,128)(2,1)S(1)}, bf16[128,768]{1,0:T(8,128)(2,1)S(1)}, u32[]{:S(2)}, u32[]{:S(2)}) collective-permute-start(bf16[128,768]{1,0:T(8,128)(2,1)S(1)} %shard_map.70), channel_id=1, source_target_pairs={{0,2},{2,0},{1,3},{3,1},{4,6},{6,4},{5,7},{7,5},{8,10},{10,8},{9,1... | collective-permute-start | bytes 589832 | tf_op jit(solution)/shard_map/ppermute | solution.py:16
  56.6 4.5 %collective-permute-start.13 = (bf16[64,128]{1,0:T(8,128)(2,1)S(1)}, bf16[64,128]{1,0:T(8,128)(2,1)S(1)}, u32[]{:S(2)}, u32[]{:S(2)}) collective-permute-start(bf16[64,128]{1,0:T(8,128)(2,1)S(1)} %get-tuple-element.53), channel_id=1, source_target_pairs={{0,4},{4,0},{8,12},{12,8},{1,5},{5,1},{9,13},{13,9},{2,6},{6,2},{1... | collective-permute-start | bytes 49160 | tf_op jit(solution)/shard_map/ppermute | solution.py:16
  58.0 4.6 %collective-permute-start.14 = (bf16[64,128]{1,0:T(8,128)(2,1)S(1)}, bf16[64,128]{1,0:T(8,128)(2,1)S(1)}, u32[]{:S(2)}, u32[]{:S(2)}) collective-permute-start(bf16[64,128]{1,0:T(8,128)(2,1)S(1)} %get-tuple-element.54), channel_id=1, source_target_pairs={{0,8},{4,12},{8,0},{12,4},{1,9},{5,13},{9,1},{13,5},{2,10},{6,14},... | collective-permute-start | bytes 49160 | tf_op jit(solution)/shard_map/ppermute | solution.py:16
  59.1 5.5 %collective-permute-start.15 = (bf16[64,128]{1,0:T(8,128)(2,1)S(1)}, bf16[64,128]{1,0:T(8,128)(2,1)S(1)}, u32[]{:S(2)}, u32[]{:S(2)}) collective-permute-start(bf16[64,128]{1,0:T(8,128)(2,1)S(1)} %get-tuple-element.55), channel_id=1, source_target_pairs={{0,12},{4,8},{8,4},{12,0},{1,13},{5,9},{9,5},{13,1},{2,14},{6,10},... | collective-permute-start | bytes 49160 | tf_op jit(solution)/shard_map/ppermute | solution.py:16
  64.6 4.3 %collective-permute-start.18 = (bf16[4,64,128]{2,1,0:T(8,128)(2,1)S(1)}, bf16[4,64,128]{2,1,0:T(8,128)(2,1)S(1)}, u32[]{:S(2)}, u32[]{:S(2)}) collective-permute-start(bf16[4,64,128]{2,1,0:T(8,128)(2,1)S(1)} %shard_map.73.mine_ref), channel_id=1, source_target_pairs={{0,2},{2,0},{1,3},{3,1},{4,6},{6,4},{5,7},{7,5},{8,10},{10,8},{9,1... | collective-permute-start | bytes 196616 | tf_op jit(solution)/shard_map/ppermute | solution.py:16
  65.9 3.4 %collective-permute-start.16 = (bf16[4,64,128]{2,1,0:T(8,128)(2,1)S(1)}, bf16[4,64,128]{2,1,0:T(8,128)(2,1)S(1)}, u32[]{:S(2)}, u32[]{:S(2)}) collective-permute-start(bf16[4,64,128]{2,1,0:T(8,128)(2,1)S(1)} %shard_map.73.mine_ref), channel_id=1, source_target_pairs={{0,1},{1,0},{2,3},{3,2},{4,5},{5,4},{6,7},{7,6},{8,9},{9,8},{10,11... | collective-permute-start | bytes 196616 | tf_op jit(solution)/shard_map/ppermute | solution.py:16
  68.9 1.3 %collective-permute-start.19 = (bf16[4,64,128]{2,1,0:T(8,128)(2,1)S(1)}, bf16[4,64,128]{2,1,0:T(8,128)(2,1)S(1)}, u32[]{:S(2)}, u32[]{:S(2)}) collective-permute-start(bf16[4,64,128]{2,1,0:T(8,128)(2,1)S(1)} %collective-permute-done.18.mine2_ref), channel_id=1, source_target_pairs={{0,1},{1,0},{2,3},{3,2},{4,5},{5,4},{6,7},{7,6},{8,9},{9,8},{10,11... | collective-permute-start | bytes 196616 | tf_op jit(solution)/shard_map/ppermute | solution.py:16

commit v3 on v2

--- a/solution.py
+++ b/solution.py
@@ -10,6 +10,8 @@
 
 HD = 128
 MIB = 1 << 20
+PACK_MIB = 52.5
+FETCH_MIB = 48
 
 
 def swapped(array, axis, bits):
@@ -25,7 +27,7 @@
         in_specs=[pl.BlockSpec(memory_space=space) for space in spaces],
         out_specs=[pl.BlockSpec(memory_space=pltpu.VMEM)] * len(outs),
         scratch_shapes=scratch,
-        compiler_params=pltpu.CompilerParams(vmem_limit_bytes=limit * MIB),
+        compiler_params=pltpu.CompilerParams(vmem_limit_bytes=int(limit * MIB)),
         cost_estimate=pl.CostEstimate(flops=flops, bytes_accessed=moved, transcendentals=0),
     )(*args)
 
@@ -34,29 +36,39 @@
     return pl.ds(pl.multiple_of(head * HD, HD), count * HD)
 
 
-def start_all(copies, sem):
-    copies = [pltpu.make_async_copy(src, dst, sem.at[i]) for i, (src, dst) in enumerate(copies)]
+def pack_body(slots, per, chunks, q_ref, k_ref, v_ref, *refs):
+    outs, (held_ref, sem) = refs[:-2], refs[-2:]
+    place = lax.axis_index("seq")
+    copies = [
+        pltpu.make_async_copy(ref, held_ref.at[part], sem.at[part])
+        for part, ref in enumerate((q_ref, k_ref, v_ref))
+    ]
     for copy in copies:
         copy.start()
-    for copy in copies:
+    for part, copy in enumerate(copies):
         copy.wait()
-
-
-def pack_body(slots, per, chunks, q_ref, k_ref, v_ref, *refs):
+        for index, (first, count) in enumerate(chunks):
+            for slot in range(slots):
+                cols = columns((place ^ slot) * per + first, count)
+                outs[index * slots + slot][part] = held_ref[part, :, cols]
+
+
+def bias_body(slots, per, mask_ref, guidance_ref, bias_ref, strength_ref):
+    place = lax.axis_index("seq")
+    rows = bias_ref.shape[1] // slots
+    for head in range(per):
+        for slot in range(slots):
+            for other in range(slots):
+                listed = mask_ref[place ^ slot, place ^ other, place * per + head]
+                offset = jnp.where((listed > 0) | (slot == other), 0.0, -1e30).astype(jnp.float32)
+                line = head * slots + slot
+                bias_ref[line : line + 1, other * rows : (other + 1) * rows] = jnp.full((1, rows), offset)
+    strength_ref[...] = jnp.full(strength_ref.shape, guidance_ref[0])
+
+
+def fetch_body(slots, per, chunks, w_ref, *refs):
     outs, sem = refs[:-1], refs[-1]
-    place = lax.axis_index("seq")
-    copies = []
-    for index, (first, count) in enumerate(chunks):
-        for slot in range(slots):
-            cols = columns((place ^ slot) * per + first, count)
-            for part, ref in enumerate((q_ref, k_ref, v_ref)):
-                copies.append((ref.at[:, cols], outs[index * slots + slot].at[part]))
-    start_all(copies, sem)
-
-
-def setup_body(slots, per, chunks, w_ref, mask_ref, guidance_ref, *refs):
-    outs, (bias_ref, strength_ref, sem) = refs[:-3], refs[-3:]
-    place, side = lax.axis_index("seq"), lax.axis_index("head")
+    side = lax.axis_index("head")
     width = outs[0].shape[1]
     copies = []
     for index, (first, count) in enumerate(chunks):
@@ -69,21 +81,12 @@
     copies = [pltpu.make_async_copy(src, dst, sem.at[i]) for i, (src, dst) in enumerate(copies)]
     for copy in copies:
         copy.start()
-    rows = bias_ref.shape[1] // slots
-    for head in range(per):
-        for slot in range(slots):
-            for other in range(slots):
-                listed = mask_ref[place ^ slot, place ^ other, place * per + head]
-                offset = jnp.where((listed > 0) | (slot == other), 0.0, -1e30).astype(jnp.float32)
-                line = head * slots + slot
-                bias_ref[line : line + 1, other * rows : (other + 1) * rows] = jnp.full((1, rows), offset)
-    strength_ref[...] = jnp.full(strength_ref.shape, guidance_ref[0])
     for copy in copies:
         copy.wait()
 
 
 def attend_body(slots, first, count, scale, bias_ref, *refs):
-    blocks, (keep_ref, send_ref) = refs[:slots], refs[slots:]
+    blocks, outs = refs[:slots], refs[slots:]
     rows = blocks[0].shape[1]
     half = rows // 2
     low = lax.axis_index("cfg") == 0
@@ -103,8 +106,11 @@
             total = jnp.sum(expo, axis=1, keepdims=True)
             out = jnp.dot(expo.astype(jnp.bfloat16), values, preferred_element_type=jnp.float32)
             out = (out / total).astype(jnp.bfloat16)
-            keep_ref[slot, :, cols] = jnp.where(low, out[:half], out[half:])
-            send_ref[slot, :, cols] = jnp.where(low, out[half:], out[:half])
+            if len(outs) == 1:
+                outs[0][slot, :, cols] = out
+            else:
+                outs[0][slot, :, cols] = jnp.where(low, out[:half], out[half:])
+                outs[1][slot, :, cols] = jnp.where(low, out[half:], out[:half])
 
 
 def guide_body(slots, scale_ref, own_ref, other_ref, *outs):
@@ -124,7 +130,7 @@
         out[slot] = ins[slot][...]
 
 
-def spread(wide_ref, slots, mine_ref, theirs_ref):
+def early_body(slots, keep_ref, send_ref, mine_ref, theirs_ref, kept_ref, sent_ref, wide_ref):
     place, core = lax.axis_index("seq"), lax.axis_index("cfg")
     half = mine_ref.shape[1]
     count = mine_ref.shape[2] // HD
@@ -132,21 +138,22 @@
         cols = columns((place ^ slot) * count, count)
         wide_ref[pl.ds(pl.multiple_of(core * half, half), half), cols] = mine_ref[slot]
         wide_ref[pl.ds(pl.multiple_of((1 - core) * half, half), half), cols] = theirs_ref[slot]
-
-
-def project_body(slots, w_ref, mine_ref, theirs_ref, out_ref, wide_ref):
-    spread(wide_ref, slots, mine_ref, theirs_ref)
-    out_ref[...] = jnp.dot(
-        wide_ref[...], w_ref[...], preferred_element_type=jnp.float32
-    ).astype(out_ref.dtype)
-
-
-def finish_body(slots, sum_ref, part_ref, w_ref, mine_ref, theirs_ref, w2_ref, mine2_ref, theirs2_ref, out_ref, wide_ref):
-    total = sum_ref[...] + part_ref[...].astype(jnp.float32)
-    for w, mine, theirs in ((w_ref, mine_ref, theirs_ref), (w2_ref, mine2_ref, theirs2_ref)):
-        spread(wide_ref, slots, mine, theirs)
-        total += jnp.dot(wide_ref[...], w[...], preferred_element_type=jnp.float32)
-    out_ref[...] = total.astype(out_ref.dtype)
+    for w_ref, out_ref in ((send_ref, sent_ref), (keep_ref, kept_ref)):
+        out_ref[...] = jnp.dot(wide_ref[...], w_ref[...], preferred_element_type=jnp.float32)
+
+
+def late_body(slots, w_ref, sum_ref, *refs):
+    blocks, (out_ref, wide_ref) = refs[:slots], refs[slots:]
+    place = lax.axis_index("seq")
+    count = blocks[0].shape[1] // HD
+    for slot in range(slots):
+        wide_ref[:, columns((place ^ slot) * count, count)] = blocks[slot][...]
+    terms = jnp.dot(wide_ref[...], w_ref[...], preferred_element_type=jnp.float32)
+    out_ref[...] = (sum_ref[...] + terms).astype(out_ref.dtype)
+
+
+def add_body(left_ref, right_ref, out_ref):
+    out_ref[...] = (left_ref[...] + right_ref[...].astype(jnp.float32)).astype(out_ref.dtype)
 
 
 def by_heads(queries, keys, values, band_mask, out_weight, guidance):
@@ -167,10 +174,10 @@
         [own_q, own_k, own_v],
         0,
         spaces=[pltpu.HBM] * 3,
-        scratch=[pltpu.SemaphoreType.DMA((3 * slots * len(chunks),))],
-        limit=53,
-    )
-    order = sorted(range(1, slots), reverse=True)
+        scratch=[pltpu.VMEM((3, rows, wide), bf16), pltpu.SemaphoreType.DMA((3,))],
+        limit=PACK_MIB,
+    )
+    order = partners(slots)
     received = []
     for index in range(len(chunks)):
         got = {0: packed[index * slots]}
@@ -178,68 +185,79 @@
             got[slot] = swapped(packed[index * slots + slot], "seq", slot)
         received.append([got[s] for s in range(slots)])
 
-    *weights, bias, strength = call(
-        functools.partial(setup_body, slots, per, chunks),
-        [shape((slots * c * HD, width), bf16) for _, c in chunks for _ in range(2)]
-        + [shape((per * slots, slots * rows), f32), shape((8, HD), f32)],
-        [out_weight, jnp.transpose(band_mask, (1, 2, 0)), guidance],
+    bias, strength = call(
+        functools.partial(bias_body, slots, per),
+        [shape((per * slots, slots * rows), f32), shape((8, HD), f32)],
+        [jnp.transpose(band_mask, (1, 2, 0)), guidance],
+        0,
+        spaces=[pltpu.SMEM, pltpu.SMEM],
+    )
+    keep0, send0, keep1, send1 = call(
+        functools.partial(fetch_body, slots, per, chunks),
+        [shape((slots * c * HD, width), bf16) for _, c in chunks for _ in range(2)],
+        [out_weight],
         10**9,
-        spaces=[pltpu.HBM, pltpu.SMEM, pltpu.SMEM],
+        spaces=[pltpu.HBM],
         scratch=[pltpu.SemaphoreType.DMA((2 * slots * len(chunks),))],
-    )
-    keep0, send0, keep1, send1 = weights
-    other1 = swapped(send1, "head", 1)
-
-    shared = []
-    for (first, count), blocks in zip(chunks, received):
-        block = shape((slots, half, count * HD), bf16)
-        keep, send = call(
+        limit=FETCH_MIB,
+    )
+
+    backs = []
+    for index, ((first, count), blocks) in enumerate(zip(chunks, received)):
+        part = half if index == 0 else rows
+        attended = call(
             functools.partial(attend_body, slots, first, count, HD ** (-0.5)),
-            [block, block],
+            [shape((slots, part, count * HD), bf16)] * (2 - index),
             [bias, *blocks],
             4 * count * (slots * rows) ** 2 * HD,
         )
-        other = swapped(send, "cfg", 1)
+        other = swapped(attended[-1], "cfg", 1)
         guided = call(
             functools.partial(guide_body, slots),
-            [shape((half, count * HD), bf16)] * slots,
-            [strength, keep, other],
-            8 * slots * half * count * HD,
+            [shape((part, count * HD), bf16)] * slots,
+            [strength, attended[0], other],
+            8 * slots * part * count * HD,
         )
         back = {0: guided[0]}
         for slot in order:
             back[slot] = swapped(guided[slot], "seq", slot)
-        (mine,) = call(
-            functools.partial(join_body, slots), [block],
-            [back[s] for s in range(slots)], 0,
-        )
-        shared.append((mine, swapped(mine, "cfg", 1)))
-    (mine0, theirs0), (mine1, theirs1) = shared
-
-    def project(weight, dtype):
+        backs.append([back[s] for s in range(slots)])
+
+    (mine0,) = call(
+        functools.partial(join_body, slots), [shape((slots, half, chunks[0][1] * HD), bf16)],
+        backs[0], 0,
+    )
+    theirs0 = swapped(mine0, "cfg", 1)
+    depth = keep0.shape[0]
+    kept0, sent0 = call(
+        functools.partial(early_body, slots),
+        [shape((rows, width), f32)] * 2,
+        [keep0, send0, mine0, theirs0],
+        4 * rows * depth * width,
+        scratch=[pltpu.VMEM((rows, depth), bf16)],
+    )
+
+    def late(weight, total, dtype):
         depth = weight.shape[0]
         (out,) = call(
-            functools.partial(project_body, slots),
+            functools.partial(late_body, slots),
             [shape((rows, width), dtype)],
-            [weight, mine0, theirs0],
+            [weight, total, *backs[1]],
             2 * rows * depth * width,
             scratch=[pltpu.VMEM((rows, depth), bf16)],
         )
         return out
 
-    part = swapped(project(send0, bf16), "head", 1)
-    total = project(keep0, f32)
-    mine2 = swapped(mine1, "head", 1)
-    theirs2 = swapped(mine2, "cfg", 1)
-    depth = keep1.shape[0]
+    part = swapped(late(send1, sent0, bf16), "head", 1)
     (out,) = call(
-        functools.partial(finish_body, slots),
-        [shape((rows, width), bf16)],
-        [total, part, keep1, mine1, theirs1, other1, mine2, theirs2],
-        4 * rows * depth * width,
-        scratch=[pltpu.VMEM((rows, depth), bf16)],
+        add_body, [shape((rows, width), bf16)],
+        [late(keep1, kept0, f32), part], rows * width,
     )
     return out
+
+
+def partners(slots):
+    return [s for s in range(1, slots) if s >= slots // 2] + list(range(1, slots // 2))[::-1]
 
 
 def by_bands(queries, keys, values, band_mask, out_weight, guidance):

time: 71.5 us -> 60.3 us (0.84)
  waiting for transfers between devices: 35.4 us -> 26.2 us
  local copies, waits for them, and re-layouts: 3.03 us -> 0.69 us
  Pallas kernels: 8.83 us -> 10 us
  starting transfers between devices: 23.2 us -> 22.3 us
    ppermute x20 -> x16, waiting for transfers between devices: 35.4 us -> 26.2 us  [swapped(): lax.ppermute(array, axis, [(i, i ^ bits) for i in range(lax.axis_size(axi...]
    unnamed x4 -> x2, local copies, waits for them, and re-layouts: 3.03 us -> 0.69 us
    pallas_call x11 -> x12, Pallas kernels: 8.83 us -> 10 us  [call(): pl.pallas_call(body, out_shape=outs, in_specs=[pl.BlockSpec(memory_space=...]
    ppermute x20 -> x16, starting transfers between devices: 23.2 us -> 22.3 us  [swapped(): lax.ppermute(array, axis, [(i, i ^ bits) for i in range(lax.axis_size(axi...]
  transfers between devices with their start and end apart: 20 -> 16, of which waited for: 12 -> 7; matrix products, arithmetic and copies ran while one was open for 0% -> 0% of each run, Pallas kernels for 9% -> 9%
where the time goes in v3:
time: 60.3 us; the launch traced here: 60.1 us
  waiting for transfers between devices  26.2 us (43%)
  starting transfers between devices  22.3 us (37%)
  Pallas kernels  10 us (17%)
  between operations  0.79 us (1%)
  local copies, waits for them, and re-layouts  0.69 us (1%)
    ppermute x16, waiting for transfers between devices, swapped(): lax.ppermute(array, axis, [(i, i ^ bits) for i in range(lax.axis_size(axi...  26.2 us
    ppermute x16, starting transfers between devices, swapped(): lax.ppermute(array, axis, [(i, i ^ bits) for i in range(lax.axis_size(axi...  22.3 us
    pallas_call x12, Pallas kernels, call(): pl.pallas_call(body, out_shape=outs, in_specs=[pl.BlockSpec(memory_space=...  10 us
  transfers between devices with their start and end apart: 16, of which 7 were waited for; matrix products, arithmetic and copies ran while one was open for 0% of the time, Pallas kernels for 9%

profile of v3, /device:TPU:0, one launch (start us, length us, event | category | flops | bytes accessed | tf_op | source)
XLA Modules:
  0.0 60.1 jit_solution(8524370704946419526)
XLA Ops:
  0.0 1.3 %shard_map.66 = (bf16[3,128,256]{2,1,0:T(8,128)(2,1)S(1)}, bf16[3,128,256]{2,1,0:T(8,128)(2,1)S(1)}, bf16[3,128,256]{2,1,0:T(8,128)(2,1)S(1)}, bf16[3,128,256]{2...) custom-call(bf16[128,1536]{1,0:T(8,128)(2,1)} %bitcast.5, ...), custom_call_target="tpu_custom_call" | custom-call | bytes 2359296 | tf_op jit(solution)/shard_map/pallas_call | solution.py:24
  1.3 3.1 %collective-permute-start = (bf16[3,128,256]{2,1,0:T(8,128)(2,1)S(1)}, bf16[3,128,256]{2,1,0:T(8,128)(2,1)S(1)}, u32[]{:S(2)}, u32[]{:S(2)}) collective-permute-start(bf16[3,128,256]{2,1,0:T(8,128)(2,1)S(1)} %get-tuple-element.37), channel_id=1, source_target_pairs={{0,4},{4,0},{8,12},{12,8},{1,5},{5,1},{9,13},{13,9},{2,6},{6,2},{1... | collective-permute-start | bytes 589832 | tf_op jit(solution)/shard_map/ppermute | solution.py:18
  4.4 2.6 %collective-permute-start.1 = (bf16[3,128,256]{2,1,0:T(8,128)(2,1)S(1)}, bf16[3,128,256]{2,1,0:T(8,128)(2,1)S(1)}, u32[]{:S(2)}, u32[]{:S(2)}) collective-permute-start(bf16[3,128,256]{2,1,0:T(8,128)(2,1)S(1)} %get-tuple-element.38), channel_id=1, source_target_pairs={{0,8},{4,12},{8,0},{12,4},{1,9},{5,13},{9,1},{13,5},{2,10},{6,14},... | collective-permute-start | bytes 589832 | tf_op jit(solution)/shard_map/ppermute | solution.py:18
  7.7 0.7 %copy-done = s32[12,4,4]{0,2,1:T(4,128)S(1)} copy-done((s32[12,4,4]{0,2,1:T(4,128)S(1)}, s32[12,4,4]{0,2,1:T(4,128)}, u32[]{:S(2)}) %copy-start) | copy-done | bytes 792
  8.4 0.8 %shard_map.65 = (f32[12,512]{1,0:T(8,128)S(1)}, f32[8,128]{1,0:T(8,128)S(1)}) custom-call(s32[4,4,12]{2,1,0:T(4,128)S(1)} %bitcast.4, f32[1]{0:T(128)S(6)} %copy.7.guidance_ref), custom_call_target="tpu_custom_call" | custom-call | bytes 29444 | tf_op jit(solution)/shard_map/pallas_call | solution.py:24
  9.1 3.7 %collective-permute-done.refs_1_ = bf16[3,128,256]{2,1,0:T(8,128)(2,1)S(1)} collective-permute-done((bf16[3,128,256]{2,1,0:T(8,128)(2,1)S(1)}, bf16[3,128,256]{2,1,0:T(8,128)(2,1)S(1)}, u32[]{:S(2)}, u32[]{:S(2)}) %collective-permute-start) | collective-permute-done | bytes 196640 | tf_op jit(solution)/shard_map/ppermute | solution.py:18
  12.8 8.7 %collective-permute-done.1.refs_2_ = bf16[3,128,256]{2,1,0:T(8,128)(2,1)S(1)} collective-permute-done((bf16[3,128,256]{2,1,0:T(8,128)(2,1)S(1)}, bf16[3,128,256]{2,1,0:T(8,128)(2,1)S(1)}, u32[]{:S(2)}, u32[]{:S(2)}) %collective-permute-start.1) | collective-permute-done | bytes 196640 | tf_op jit(solution)/shard_map/ppermute | solution.py:18
  21.5 2.2 %shard_map.67 = (bf16[4,64,256]{2,1,0:T(8,128)(2,1)S(1)}, bf16[4,64,256]{2,1,0:T(8,128)(2,1)S(1)}) custom-call(f32[12,512]{1,0:T(8,128)S(1)} %get-tuple-element.35.bias_ref, bf16[3,128,256]{2,1,0:T(8,128)(2,1)S(1)} %get-tuple-element.36.refs_0_, bf16[3,128,256]{2,1,0:T(8,128)(2,1)S(1)} %collective-permute-done.refs_1_, ...), custom_call_target="tpu_custom_call" | custom-call | flops 268435456 | bytes 1073152 | tf_op jit(solution)/shard_map/pallas_call | solution.py:24
  23.8 0.1 collective-permute-start.3
  23.9 3.5 %collective-permute-start.8 = (bf16[3,128,128]{2,1,0:T(8,128)(2,1)S(1)}, bf16[3,128,128]{2,1,0:T(8,128)(2,1)S(1)}, u32[]{:S(2)}, u32[]{:S(2)}) collective-permute-start(bf16[3,128,128]{2,1,0:T(8,128)(2,1)S(1)} %get-tuple-element.48), channel_id=1, source_target_pairs={{0,4},{4,0},{8,12},{12,8},{1,5},{5,1},{9,13},{13,9},{2,6},{6,2},{1... | collective-permute-start | bytes 294920 | tf_op jit(solution)/shard_map/ppermute | solution.py:18
  27.3 1.1 %collective-permute-start.9 = (bf16[3,128,128]{2,1,0:T(8,128)(2,1)S(1)}, bf16[3,128,128]{2,1,0:T(8,128)(2,1)S(1)}, u32[]{:S(2)}, u32[]{:S(2)}) collective-permute-start(bf16[3,128,128]{2,1,0:T(8,128)(2,1)S(1)} %get-tuple-element.49), channel_id=1, source_target_pairs={{0,8},{4,12},{8,0},{12,4},{1,9},{5,13},{9,1},{13,5},{2,10},{6,14},... | collective-permute-start | bytes 294920 | tf_op jit(solution)/shard_map/ppermute | solution.py:18
  28.4 1.4 %collective-permute-start.10 = (bf16[3,128,128]{2,1,0:T(8,128)(2,1)S(1)}, bf16[3,128,128]{2,1,0:T(8,128)(2,1)S(1)}, u32[]{:S(2)}, u32[]{:S(2)}) collective-permute-start(bf16[3,128,128]{2,1,0:T(8,128)(2,1)S(1)} %get-tuple-element.50), channel_id=1, source_target_pairs={{0,12},{4,8},{8,4},{12,0},{1,13},{5,9},{9,5},{13,1},{2,14},{6,10},... | collective-permute-start | bytes 294920 | tf_op jit(solution)/shard_map/ppermute | solution.py:18
  29.8 0.1 shard_map.68
  29.9 1.1 %collective-permute-start.4 = (bf16[64,256]{1,0:T(8,128)(2,1)S(1)}, bf16[64,256]{1,0:T(8,128)(2,1)S(1)}, u32[]{:S(2)}, u32[]{:S(2)}) collective-permute-start(bf16[64,256]{1,0:T(8,128)(2,1)S(1)} %get-tuple-element.43), channel_id=1, source_target_pairs={{0,4},{4,0},{8,12},{12,8},{1,5},{5,1},{9,13},{13,9},{2,6},{6,2},{1... | collective-permute-start | bytes 98312 | tf_op jit(solution)/shard_map/ppermute | solution.py:18
  31.0 2.0 %collective-permute-start.5 = (bf16[64,256]{1,0:T(8,128)(2,1)S(1)}, bf16[64,256]{1,0:T(8,128)(2,1)S(1)}, u32[]{:S(2)}, u32[]{:S(2)}) collective-permute-start(bf16[64,256]{1,0:T(8,128)(2,1)S(1)} %get-tuple-element.44), channel_id=1, source_target_pairs={{0,8},{4,12},{8,0},{12,4},{1,9},{5,13},{9,1},{13,5},{2,10},{6,14},... | collective-permute-start | bytes 98312 | tf_op jit(solution)/shard_map/ppermute | solution.py:18
  33.0 1.4 %collective-permute-start.6 = (bf16[64,256]{1,0:T(8,128)(2,1)S(1)}, bf16[64,256]{1,0:T(8,128)(2,1)S(1)}, u32[]{:S(2)}, u32[]{:S(2)}) collective-permute-start(bf16[64,256]{1,0:T(8,128)(2,1)S(1)} %get-tuple-element.45), channel_id=1, source_target_pairs={{0,12},{4,8},{8,4},{12,0},{1,13},{5,9},{9,5},{13,1},{2,14},{6,10},... | collective-permute-start | bytes 98312 | tf_op jit(solution)/shard_map/ppermute | solution.py:18
  34.4 5.1 %collective-permute-done.9.refs_2_ = bf16[3,128,128]{2,1,0:T(8,128)(2,1)S(1)} collective-permute-done((bf16[3,128,128]{2,1,0:T(8,128)(2,1)S(1)}, bf16[3,128,128]{2,1,0:T(8,128)(2,1)S(1)}, u32[]{:S(2)}, u32[]{:S(2)}) %collective-permute-start.9) | collective-permute-done | bytes 98336 | tf_op jit(solution)/shard_map/ppermute | solution.py:18
  39.5 1.2 %shard_map.71.own_ref = bf16[4,128,128]{2,1,0:T(8,128)(2,1)S(1)} custom-call(f32[12,512]{1,0:T(8,128)S(1)} %get-tuple-element.35.bias_ref, bf16[3,128,128]{2,1,0:T(8,128)(2,1)S(1)} %get-tuple-element.47.refs_0_, bf16[3,128,128]{2,1,0:T(8,128)(2,1)S(1)} %collective-permute-done.8.refs_1_, bf16[3,128,128]{2,1,0:T(8,128)(2,1)S(1)} %collective-permute-done.9.refs_2_, ...), custom_call_target="tpu_custom_call" | custom-call | flops 134217728 | bytes 548864 | tf_op jit(solution)/shard_map/pallas_call | solution.py:24
  40.8 1.1 %collective-permute-done.5.refs_2_ = bf16[64,256]{1,0:T(8,128)(2,1)S(1)} collective-permute-done((bf16[64,256]{1,0:T(8,128)(2,1)S(1)}, bf16[64,256]{1,0:T(8,128)(2,1)S(1)}, u32[]{:S(2)}, u32[]{:S(2)}) %collective-permute-start.5) | collective-permute-done | bytes 32800 | tf_op jit(solution)/shard_map/ppermute | solution.py:18
  42.0 2.4 %shard_map.64 = (bf16[1024,768]{1,0:T(8,128)(2,1)S(1)}, bf16[1024,768]{1,0:T(8,128)(2,1)S(1)}, bf16[512,768]{1,0:T(8,128)(2,1)S(1)}, bf16[512,768]{1,0:T(8,128)(2,1)S(1)}) custom-call(bf16[1536,1536]{1,0:T(8,128)(2,1)} %w_ref.1), custom_call_target="tpu_custom_call" | custom-call | flops 1000000000 | bytes 9437184 | tf_op jit(solution)/shard_map/pallas_call | solution.py:24
  44.4 0.1 shard_map.72
  44.5 2.0 %collective-permute-start.12 = (bf16[128,128]{1,0:T(8,128)(2,1)S(1)}, bf16[128,128]{1,0:T(8,128)(2,1)S(1)}, u32[]{:S(2)}, u32[]{:S(2)}) collective-permute-start(bf16[128,128]{1,0:T(8,128)(2,1)S(1)} %get-tuple-element.52), channel_id=1, source_target_pairs={{0,4},{4,0},{8,12},{12,8},{1,5},{5,1},{9,13},{13,9},{2,6},{6,2},{1... | collective-permute-start | bytes 98312 | tf_op jit(solution)/shard_map/ppermute | solution.py:18
  46.6 1.1 %collective-permute-start.13 = (bf16[128,128]{1,0:T(8,128)(2,1)S(1)}, bf16[128,128]{1,0:T(8,128)(2,1)S(1)}, u32[]{:S(2)}, u32[]{:S(2)}) collective-permute-start(bf16[128,128]{1,0:T(8,128)(2,1)S(1)} %get-tuple-element.53), channel_id=1, source_target_pairs={{0,8},{4,12},{8,0},{12,4},{1,9},{5,13},{9,1},{13,5},{2,10},{6,14},... | collective-permute-start | bytes 98312 | tf_op jit(solution)/shard_map/ppermute | solution.py:18
  47.6 1.4 %collective-permute-start.14 = (bf16[128,128]{1,0:T(8,128)(2,1)S(1)}, bf16[128,128]{1,0:T(8,128)(2,1)S(1)}, u32[]{:S(2)}, u32[]{:S(2)}) collective-permute-start(bf16[128,128]{1,0:T(8,128)(2,1)S(1)} %get-tuple-element.54), channel_id=1, source_target_pairs={{0,12},{4,8},{8,4},{12,0},{1,13},{5,9},{9,5},{13,1},{2,14},{6,10},... | collective-permute-start | bytes 98312 | tf_op jit(solution)/shard_map/ppermute | solution.py:18
  49.0 0.6 shard_map.70
  49.6 2.2 %collective-permute-done.13.refs_2_ = bf16[128,128]{1,0:T(8,128)(2,1)S(1)} collective-permute-done((bf16[128,128]{1,0:T(8,128)(2,1)S(1)}, bf16[128,128]{1,0:T(8,128)(2,1)S(1)}, u32[]{:S(2)}, u32[]{:S(2)}) %collective-permute-start.13) | collective-permute-done | bytes 32800 | tf_op jit(solution)/shard_map/ppermute | solution.py:18
  51.8 1.5 %collective-permute-done.14.refs_3_ = bf16[128,128]{1,0:T(8,128)(2,1)S(1)} collective-permute-done((bf16[128,128]{1,0:T(8,128)(2,1)S(1)}, bf16[128,128]{1,0:T(8,128)(2,1)S(1)}, u32[]{:S(2)}, u32[]{:S(2)}) %collective-permute-start.14) | collective-permute-done | bytes 32800 | tf_op jit(solution)/shard_map/ppermute | solution.py:18
  53.3 0.3 shard_map.74
  53.6 1.6 %collective-permute-start.15 = (bf16[128,768]{1,0:T(8,128)(2,1)S(1)}, bf16[128,768]{1,0:T(8,128)(2,1)S(1)}, u32[]{:S(2)}, u32[]{:S(2)}) collective-permute-start(bf16[128,768]{1,0:T(8,128)(2,1)S(1)} %shard_map.74), channel_id=1, source_target_pairs={{0,2},{2,0},{1,3},{3,1},{4,6},{6,4},{5,7},{7,5},{8,10},{10,8},{9,1... | collective-permute-start | bytes 589832 | tf_op jit(solution)/shard_map/ppermute | solution.py:18
  55.2 0.3 shard_map.73.left_ref
  55.5 3.9 %collective-permute-done.15.right_ref = bf16[128,768]{1,0:T(8,128)(2,1)S(1)} collective-permute-done((bf16[128,768]{1,0:T(8,128)(2,1)S(1)}, bf16[128,768]{1,0:T(8,128)(2,1)S(1)}, u32[]{:S(2)}, u32[]{:S(2)}) %collective-permute-start.15) | collective-permute-done | bytes 196640 | tf_op jit(solution)/shard_map/ppermute | solution.py:18
  59.4 0.7 %shard_map.75 = bf16[128,768]{1,0:T(8,128)(2,1)} custom-call(f32[128,768]{1,0:T(8,128)S(1)} %shard_map.73.left_ref, bf16[128,768]{1,0:T(8,128)(2,1)S(1)} %collective-permute-done.15.right_ref), custom_call_target="tpu_custom_call" | custom-call | flops 98304 | bytes 786432 | tf_op jit(solution)/shard_map/pallas_call | solution.py:24
  (14 shorter events, 0.2 us)
Async XLA Ops:
  1.3 11.5 %collective-permute-start = (bf16[3,128,256]{2,1,0:T(8,128)(2,1)S(1)}, bf16[3,128,256]{2,1,0:T(8,128)(2,1)S(1)}, u32[]{:S(2)}, u32[]{:S(2)}) collective-permute-start(bf16[3,128,256]{2,1,0:T(8,128)(2,1)S(1)} %get-tuple-element.37), channel_id=1, source_target_pairs={{0,4},{4,0},{8,12},{12,8},{1,5},{5,1},{9,13},{13,9},{2,6},{6,2},{1... | collective-permute-start | bytes 589832 | tf_op jit(solution)/shard_map/ppermute | solution.py:18
  4.4 17.1 %collective-permute-start.1 = (bf16[3,128,256]{2,1,0:T(8,128)(2,1)S(1)}, bf16[3,128,256]{2,1,0:T(8,128)(2,1)S(1)}, u32[]{:S(2)}, u32[]{:S(2)}) collective-permute-start(bf16[3,128,256]{2,1,0:T(8,128)(2,1)S(1)} %get-tuple-element.38), channel_id=1, source_target_pairs={{0,8},{4,12},{8,0},{12,4},{1,9},{5,13},{9,1},{13,5},{2,10},{6,14},... | collective-permute-start | bytes 589832 | tf_op jit(solution)/shard_map/ppermute | solution.py:18
  7.0 14.5 %collective-permute-start.2 = (bf16[3,128,256]{2,1,0:T(8,128)(2,1)S(1)}, bf16[3,128,256]{2,1,0:T(8,128)(2,1)S(1)}, u32[]{:S(2)}, u32[]{:S(2)}) collective-permute-start(bf16[3,128,256]{2,1,0:T(8,128)(2,1)S(1)} %get-tuple-element.39), channel_id=1, source_target_pairs={{0,12},{4,8},{8,4},{12,0},{1,13},{5,9},{9,5},{13,1},{2,14},{6,10},... | collective-permute-start | bytes 589832 | tf_op jit(solution)/shard_map/ppermute | solution.py:18
  7.7 0.7 %copy-start = (s32[12,4,4]{0,2,1:T(4,128)S(1)}, s32[12,4,4]{0,2,1:T(4,128)}, u32[]{:S(2)}) copy-start(s32[12,4,4]{0,2,1:T(4,128)} %param.9) | copy-start | bytes 2308
  23.8 6.0 %collective-permute-start.3 = (bf16[4,64,256]{2,1,0:T(8,128)(2,1)S(1)}, bf16[4,64,256]{2,1,0:T(8,128)(2,1)S(1)}, u32[]{:S(2)}, u32[]{:S(2)}) collective-permute-start(bf16[4,64,256]{2,1,0:T(8,128)(2,1)S(1)} %get-tuple-element.41), channel_id=1, source_target_pairs={{0,1},{1,0},{2,3},{3,2},{4,5},{5,4},{6,7},{7,6},{8,9},{9,8},{10,11... | collective-permute-start | bytes 393224 | tf_op jit(solution)/shard_map/ppermute | solution.py:18
  23.9 9.1 %collective-permute-start.8 = (bf16[3,128,128]{2,1,0:T(8,128)(2,1)S(1)}, bf16[3,128,128]{2,1,0:T(8,128)(2,1)S(1)}, u32[]{:S(2)}, u32[]{:S(2)}) collective-permute-start(bf16[3,128,128]{2,1,0:T(8,128)(2,1)S(1)} %get-tuple-element.48), channel_id=1, source_target_pairs={{0,4},{4,0},{8,12},{12,8},{1,5},{5,1},{9,13},{13,9},{2,6},{6,2},{1... | collective-permute-start | bytes 294920 | tf_op jit(solution)/shard_map/ppermute | solution.py:18
  27.3 12.2 %collective-permute-start.9 = (bf16[3,128,128]{2,1,0:T(8,128)(2,1)S(1)}, bf16[3,128,128]{2,1,0:T(8,128)(2,1)S(1)}, u32[]{:S(2)}, u32[]{:S(2)}) collective-permute-start(bf16[3,128,128]{2,1,0:T(8,128)(2,1)S(1)} %get-tuple-element.49), channel_id=1, source_target_pairs={{0,8},{4,12},{8,0},{12,4},{1,9},{5,13},{9,1},{13,5},{2,10},{6,14},... | collective-permute-start | bytes 294920 | tf_op jit(solution)/shard_map/ppermute | solution.py:18
  28.4 11.1 %collective-permute-start.10 = (bf16[3,128,128]{2,1,0:T(8,128)(2,1)S(1)}, bf16[3,128,128]{2,1,0:T(8,128)(2,1)S(1)}, u32[]{:S(2)}, u32[]{:S(2)}) collective-permute-start(bf16[3,128,128]{2,1,0:T(8,128)(2,1)S(1)} %get-tuple-element.50), channel_id=1, source_target_pairs={{0,12},{4,8},{8,4},{12,0},{1,13},{5,9},{9,5},{13,1},{2,14},{6,10},... | collective-permute-start | bytes 294920 | tf_op jit(solution)/shard_map/ppermute | solution.py:18
  29.9 10.9 %collective-permute-start.4 = (bf16[64,256]{1,0:T(8,128)(2,1)S(1)}, bf16[64,256]{1,0:T(8,128)(2,1)S(1)}, u32[]{:S(2)}, u32[]{:S(2)}) collective-permute-start(bf16[64,256]{1,0:T(8,128)(2,1)S(1)} %get-tuple-element.43), channel_id=1, source_target_pairs={{0,4},{4,0},{8,12},{12,8},{1,5},{5,1},{9,13},{13,9},{2,6},{6,2},{1... | collective-permute-start | bytes 98312 | tf_op jit(solution)/shard_map/ppermute | solution.py:18
  31.0 10.9 %collective-permute-start.5 = (bf16[64,256]{1,0:T(8,128)(2,1)S(1)}, bf16[64,256]{1,0:T(8,128)(2,1)S(1)}, u32[]{:S(2)}, u32[]{:S(2)}) collective-permute-start(bf16[64,256]{1,0:T(8,128)(2,1)S(1)} %get-tuple-element.44), channel_id=1, source_target_pairs={{0,8},{4,12},{8,0},{12,4},{1,9},{5,13},{9,1},{13,5},{2,10},{6,14},... | collective-permute-start | bytes 98312 | tf_op jit(solution)/shard_map/ppermute | solution.py:18
  33.0 8.9 %collective-permute-start.6 = (bf16[64,256]{1,0:T(8,128)(2,1)S(1)}, bf16[64,256]{1,0:T(8,128)(2,1)S(1)}, u32[]{:S(2)}, u32[]{:S(2)}) collective-permute-start(bf16[64,256]{1,0:T(8,128)(2,1)S(1)} %get-tuple-element.45), channel_id=1, source_target_pairs={{0,12},{4,8},{8,4},{12,0},{1,13},{5,9},{9,5},{13,1},{2,14},{6,10},... | collective-permute-start | bytes 98312 | tf_op jit(solution)/shard_map/ppermute | solution.py:18
  40.7 3.7 %collective-permute-start.11 = (bf16[4,128,128]{2,1,0:T(8,128)(2,1)S(1)}, bf16[4,128,128]{2,1,0:T(8,128)(2,1)S(1)}, u32[]{:S(2)}, u32[]{:S(2)}) collective-permute-start(bf16[4,128,128]{2,1,0:T(8,128)(2,1)S(1)} %shard_map.71.own_ref), channel_id=1, source_target_pairs={{0,1},{1,0},{2,3},{3,2},{4,5},{5,4},{6,7},{7,6},{8,9},{9,8},{10,11... | collective-permute-start | bytes 393224 | tf_op jit(solution)/shard_map/ppermute | solution.py:18
  41.9 7.1 %collective-permute-start.7 = (bf16[4,64,256]{2,1,0:T(8,128)(2,1)S(1)}, bf16[4,64,256]{2,1,0:T(8,128)(2,1)S(1)}, u32[]{:S(2)}, u32[]{:S(2)}) collective-permute-start(bf16[4,64,256]{2,1,0:T(8,128)(2,1)S(1)} %shard_map.69.mine_ref), channel_id=1, source_target_pairs={{0,1},{1,0},{2,3},{3,2},{4,5},{5,4},{6,7},{7,6},{8,9},{9,8},{10,11... | collective-permute-start | bytes 393224 | tf_op jit(solution)/shard_map/ppermute | solution.py:18
  44.5 5.1 %collective-permute-start.12 = (bf16[128,128]{1,0:T(8,128)(2,1)S(1)}, bf16[128,128]{1,0:T(8,128)(2,1)S(1)}, u32[]{:S(2)}, u32[]{:S(2)}) collective-permute-start(bf16[128,128]{1,0:T(8,128)(2,1)S(1)} %get-tuple-element.52), channel_id=1, source_target_pairs={{0,4},{4,0},{8,12},{12,8},{1,5},{5,1},{9,13},{13,9},{2,6},{6,2},{1... | collective-permute-start | bytes 98312 | tf_op jit(solution)/shard_map/ppermute | solution.py:18
  46.6 5.2 %collective-permute-start.13 = (bf16[128,128]{1,0:T(8,128)(2,1)S(1)}, bf16[128,128]{1,0:T(8,128)(2,1)S(1)}, u32[]{:S(2)}, u32[]{:S(2)}) collective-permute-start(bf16[128,128]{1,0:T(8,128)(2,1)S(1)} %get-tuple-element.53), channel_id=1, source_target_pairs={{0,8},{4,12},{8,0},{12,4},{1,9},{5,13},{9,1},{13,5},{2,10},{6,14},... | collective-permute-start | bytes 98312 | tf_op jit(solution)/shard_map/ppermute | solution.py:18
  47.6 5.7 %collective-permute-start.14 = (bf16[128,128]{1,0:T(8,128)(2,1)S(1)}, bf16[128,128]{1,0:T(8,128)(2,1)S(1)}, u32[]{:S(2)}, u32[]{:S(2)}) collective-permute-start(bf16[128,128]{1,0:T(8,128)(2,1)S(1)} %get-tuple-element.54), channel_id=1, source_target_pairs={{0,12},{4,8},{8,4},{12,0},{1,13},{5,9},{9,5},{13,1},{2,14},{6,10},... | collective-permute-start | bytes 98312 | tf_op jit(solution)/shard_map/ppermute | solution.py:18
  53.6 5.7 %collective-permute-start.15 = (bf16[128,768]{1,0:T(8,128)(2,1)S(1)}, bf16[128,768]{1,0:T(8,128)(2,1)S(1)}, u32[]{:S(2)}, u32[]{:S(2)}) collective-permute-start(bf16[128,768]{1,0:T(8,128)(2,1)S(1)} %shard_map.74), channel_id=1, source_target_pairs={{0,2},{2,0},{1,3},{3,1},{4,6},{6,4},{5,7},{7,5},{8,10},{10,8},{9,1... | collective-permute-start | bytes 589832 | tf_op jit(solution)/shard_map/ppermute | solution.py:18
